TPU v7x, 128 devices: a whole 4x4x4 slice. The times are simulated.
128 devices in a mesh: gx: 16 (over y, x), gy: 8 (over z, core).
Axes of the slice: x: 4, y: 4, z: 4, core: 2. Of those that a mesh axis runs over, the one named last changes fastest.
Arguments:
- queries: bfloat16 [2048, 2048], P(('gx', 'gy')), may hold values from -6 to 6
- probe_dev: int32 [2048, 16], P(('gx', 'gy')), may hold values from 0 to 127, all different within a row; in each aligned block of 16 rows (0 to 15, 16 to 31, ...) at most 2 rows name the same one
- probe_list: int32 [2048, 16], P(('gx', 'gy')), may hold values from 0 to 15
- documents: bfloat16 [2048, 256, 2048], P(('gx', 'gy')), may hold values from -6 to 6
- lengths: int32 [2048], P(('gx', 'gy')), may hold values from 96 to 256, as said below
- short_dev: int32 [2048, 32], P(('gx', 'gy')), may hold values from 0 to 127, all different within a row; in each aligned block of 16 rows (0 to 15, 16 to 31, ...) at most 5 rows name the same one
- short_list: int32 [2048, 32], P(('gx', 'gy')), may hold values from 0 to 15
- short_row: int32 [2048, 32], P(('gx', 'gy')), may hold values from 0 to 95
Outputs:
- prefix_top: float32 [2048, 32], P(('gx', 'gy'))
- rescored: float32 [2048, 32], P(('gx', 'gy'))
Inputs may be any that keep to these rules, and one draw needn't show every extreme that they name: `lengths`: every list holds at least 96 documents, and in every draw some list is full. `probe_dev`: the 16 entries of a query name different devices. Among the 16 queries of one device, no device is named more than 2 times, and some device is named exactly 2 times. `short_dev`: the 32 entries of a query name different devices. Among the 16 queries of one device, no device is named more than 5 times, and some device is named exactly 5 times.
All inputs are finite; a program needn't handle non-finite values.
Results may differ from a plain program's by a relative error of at most 0.0029.
Values may be sent and summed in bfloat16 or wider, within the bound.
A program may use at most 128 MiB of HBM per device.

v0:
```python
import jax
import jax.numpy as jnp
from jax import lax
from jax.sharding import PartitionSpec as P

PREFIX = 256
TOPK = 32


def unit_rows(values):
    return values / jnp.sqrt(1.0 + jnp.sum(values * values, axis=1, keepdims=True))


def top_values(values, count):
    return -jnp.sort(-values, axis=-1)[..., :count]


def slot_numbers(targets, count_dev):
    onehot = (targets[:, None] == jnp.arange(count_dev, dtype=jnp.int32)[None, :]).astype(jnp.int32)
    return jnp.sum(onehot * (jnp.cumsum(onehot, axis=0) - 1), axis=1)


def place_codes(position, total, codes):
    hits = position[:, None] == jnp.arange(total, dtype=jnp.int32)[None, :]
    return jnp.sum(jnp.where(hits, codes[:, None], 0), axis=0)


def place_vectors(position, total, vectors):
    hits = (position[:, None] == jnp.arange(total, dtype=jnp.int32)[None, :]).astype(jnp.bfloat16)
    placed = lax.dot_general(
        hits, vectors, (((0,), (0,)), ((), ())), preferred_element_type=jnp.float32
    )
    return placed.astype(jnp.bfloat16)


def prefix_scores(rows, documents, width):
    scores = lax.dot_general(
        rows, documents[:, :, :width], (((1,), (2,)), ((), ())), preferred_element_type=jnp.float32
    )
    return scores.reshape(rows.shape[0], -1)


def shards(queries, probe_dev, probe_list, documents, lengths, short_dev, short_list, short_row):
    query_float = queries.astype(jnp.float32)
    prefix_unit = unit_rows(query_float[:, :PREFIX]).astype(jnp.bfloat16)
    full_unit = unit_rows(query_float).astype(jnp.bfloat16)
    local_lists = documents.shape[0]
    rows_list = documents.shape[1]
    count_dev = lax.axis_size(("gx", "gy"))
    query_rows = queries.shape[0]
    probe_count = probe_dev.shape[1]
    pair_cap = min(query_rows, max(1, 4 * query_rows * probe_count // (3 * count_dev)))
    pair_dev = probe_dev.reshape(-1)
    pair_slot = slot_numbers(pair_dev, count_dev)
    pair_flat = pair_dev * pair_cap + pair_slot
    pair_prefix = jnp.repeat(prefix_unit, probe_count, axis=0)
    send_prefix = place_vectors(pair_flat, count_dev * pair_cap, pair_prefix).reshape(
        count_dev, pair_cap, PREFIX
    )
    send_list = (
        place_codes(pair_flat, count_dev * pair_cap, probe_list.reshape(-1))
        .astype(jnp.bfloat16)
        .reshape(count_dev, pair_cap)
    )
    got_prefix = lax.all_to_all(send_prefix, ("gx", "gy"), split_axis=0, concat_axis=0, tiled=True)
    got_list = lax.all_to_all(send_list, ("gx", "gy"), split_axis=0, concat_axis=0, tiled=True)
    senders = got_prefix.shape[0]
    items = got_prefix.shape[1]
    flat = got_prefix.reshape(senders * items, PREFIX)
    scores = prefix_scores(flat, documents, PREFIX).reshape(senders * items, local_lists, rows_list)
    which = (
        got_list.reshape(-1).astype(jnp.int32)[:, None]
        == jnp.arange(local_lists, dtype=jnp.int32)[None, :]
    )
    chosen = jnp.sum(jnp.where(which[:, :, None], scores, 0.0), axis=1)
    list_len = jnp.sum(jnp.where(which, lengths[None, :], 0), axis=1)
    keep_mask = jnp.arange(rows_list)[None, :] < list_len[:, None]
    best = top_values(jnp.where(keep_mask, chosen, -jnp.inf), TOPK).reshape(senders, items, TOPK)
    returned = lax.all_to_all(best, ("gx", "gy"), split_axis=0, concat_axis=0, tiled=True)
    pooled = returned.reshape(count_dev * pair_cap, TOPK)[pair_flat].reshape(
        query_rows, probe_count * TOPK
    )
    prefix_top = top_values(pooled, TOPK)
    shortlist = short_dev.shape[1]
    capacity = min(query_rows, max(1, 4 * query_rows * shortlist // (3 * count_dev)))
    targets = short_dev.reshape(-1)
    request_codes = (short_list * rows_list + short_row).reshape(-1)
    slot_ids = slot_numbers(targets, count_dev)
    flat_slots = targets * capacity + slot_ids
    requests = place_codes(flat_slots, count_dev * capacity, request_codes).reshape(
        count_dev, capacity
    )
    doc_table = documents.reshape(local_lists * rows_list, documents.shape[2])
    found_rows = doc_table[
        lax.all_to_all(requests, ("gx", "gy"), split_axis=0, concat_axis=0, tiled=True)
    ]
    fetched = lax.all_to_all(found_rows, ("gx", "gy"), split_axis=0, concat_axis=0, tiled=True)
    vectors = fetched.reshape(count_dev * capacity, -1)[flat_slots].reshape(
        query_rows, shortlist, -1
    )
    rescored = jnp.einsum("qsf,qf->qs", vectors, full_unit, preferred_element_type=jnp.float32)
    return (prefix_top, rescored)


def solution(mesh):
    in_specs = (
        P(("gx", "gy"), None),
        P(("gx", "gy"), None),
        P(("gx", "gy"), None),
        P(("gx", "gy"), None, None),
        P(("gx", "gy")),
        P(("gx", "gy"), None),
        P(("gx", "gy"), None),
        P(("gx", "gy"), None),
    )
    out_specs = (P(("gx", "gy"), None), P(("gx", "gy"), None))
    return jax.shard_map(shards, mesh=mesh, in_specs=in_specs, out_specs=out_specs, check_vma=False)
```

profile of v0, /device:TPU:1, one launch (start us, length us, event | category | flops | bytes accessed | tf_op | source)
XLA Modules:
  0.0 161.6 jit_solution(169914316860079370)
XLA Ops:
  0.7 0.8 eq.113
  1.5 0.8 reshape.232
  2.9 0.8 broadcast_in_dim.78
  3.8 0.8 convert_element_type.58
  4.6 11.5 %all-to-all-start = ((bf16[128,1,2]{2,1,0:T(2,128)(2,1)}), bf16[128,1,2]{2,1,0:T(2,128)(2,1)S(1)}, u32[]{:S(2)}, u32[]{:S(2)}) async-start(bf16[128,1,2]{2,1,0:T(2,128)(2,1)} %convert_element_type.58), calls=%async_computation | async-start | bytes 131072 | tf_op jit(solution)/shard_map/all_to_all | solution.py:66
  16.1 0.8 eq.125
  17.7 0.8 convert_element_type.52
  20.8 0.8 all_to_all.24
  21.6 3.9 %all-to-all-done = bf16[128,1,2]{2,1,0:T(2,128)(2,1)S(1)} async-done(((bf16[128,1,2]{2,1,0:T(2,128)(2,1)}), bf16[128,1,2]{2,1,0:T(2,128)(2,1)S(1)}, u32[]{:S(2)}, u32[]{:S(2)}) %all-to-all-start) | async-done | bytes 544 | tf_op jit(solution)/shard_map/all_to_all | solution.py:66
  25.5 5.8 %all-to-all-start.3 = ((s32[128,1,5]{2,1,0:T(1,128)}), s32[128,1,5]{2,1,0:T(1,128)S(1)}, u32[]{:S(2)}, u32[]{:S(2)}) async-start(s32[128,1,5]{2,1,0:T(1,128)} %bitcast.12), calls=%async_computation.3 | async-start | bytes 131072 | tf_op jit(solution)/shard_map/all_to_all | solution.py:95
  31.9 9.0 %all-to-all-done.3 = s32[128,1,5]{2,1,0:T(1,128)S(1)} async-done(((s32[128,1,5]{2,1,0:T(1,128)}), s32[128,1,5]{2,1,0:T(1,128)S(1)}, u32[]{:S(2)}, u32[]{:S(2)}) %all-to-all-start.3) | async-done | bytes 2592 | tf_op jit(solution)/shard_map/all_to_all | solution.py:95
  40.8 4.6 %all-to-all-start.1 = ((bf16[128,2,256]{2,1,0:T(2,128)(2,1)}), bf16[128,2,256]{2,1,0:T(2,128)(2,1)S(1)}, u32[]{:S(2)}, u32[]{:S(2)}) async-start(bf16[128,2,256]{2,1,0:T(2,128)(2,1)} %reshape.235), calls=%async_computation.1 | async-start | bytes 262144 | tf_op jit(solution)/shard_map/all_to_all | solution.py:65
  45.6 9.7 %all-to-all-done.1 = bf16[128,2,256]{2,1,0:T(2,128)(2,1)S(1)} async-done(((bf16[128,2,256]{2,1,0:T(2,128)(2,1)}), bf16[128,2,256]{2,1,0:T(2,128)(2,1)S(1)}, u32[]{:S(2)}, u32[]{:S(2)}) %all-to-all-start.1) | async-done | bytes 131104 | tf_op jit(solution)/shard_map/all_to_all | solution.py:65
  55.4 2.2 %select_reduce_fusion = f32[256,256]{1,0:T(8,128)S(1)} fusion(bf16[256,256,1]{1,0,2:T(8,128)(2,1)S(1)} %reshape.270, bf16[16,256,2048]{2,1,0:T(8,128)(2,1)} %param.11, pred[256,16]{0,1:T(8,128)(4,1)S(1)} %iota_compare_fusion.8), kind=kOutput, calls=%fused_computation.3 | convolution fusion | flops 538902528 | bytes 2494464 | tf_op jit(solution)/shard_map/dot_general | solution.py:37
  57.9 8.5 %sort.30 = (f32[256,256]{0,1:T(8,128)S(1)}, s32[256,256]{0,1:T(8,128)}) sort(f32[256,256]{0,1:T(8,128)S(1)} %copy.30, s32[256,256]{0,1:T(8,128)S(1)} %iota.38.clone), dimensions={1}, to_apply=%region_7.8 | sort | flops 1048576 | bytes 1048576 | tf_op jit(solution)/shard_map/jit(sort)/sort | solution.py:15
  67.2 4.3 %all-to-all-start.2 = ((f32[128,2,32]{2,1,0:T(2,128)}), f32[128,2,32]{2,1,0:T(2,128)S(1)}, u32[]{:S(2)}, u32[]{:S(2)}) async-start(f32[128,2,32]{2,1,0:T(2,128)} %bitcast.4), calls=%async_computation.2 | async-start | bytes 262144 | tf_op jit(solution)/shard_map/all_to_all | solution.py:79
  71.5 14.3 %gather_fusion.1 = bf16[640,2048]{1,0:T(8,128)(2,1)S(1)} fusion(bf16[4096,2048]{1,0:T(8,128)(2,1)} %bitcast.36, s32[1024]{0:T(1024)S(1)} %pad_clamp_fusion.1), kind=kCustom, calls=%fused_computation.1 | custom fusion | bytes 5245440 | tf_op jit(solution)/shard_map/gather | solution.py:94
  85.8 2.9 %reshape.254 = bf16[128,5,2048]{2,1,0:T(8,128)(2,1)} reshape(bf16[640,2048]{1,0:T(8,128)(2,1)S(1)} %gather_fusion.1) | data formatting | bytes 5242880 | tf_op jit(solution)/shard_map/gather | solution.py:94
  88.7 10.3 %all-to-all-start.4 = ((bf16[128,5,2048]{2,1,0:T(8,128)(2,1)}), bf16[128,5,2048]{2,1,0:T(8,128)(2,1)}, u32[]{:S(2)}, u32[]{:S(2)}) async-start(bf16[128,5,2048]{2,1,0:T(8,128)(2,1)} %reshape.254), calls=%async_computation.4 | async-start | bytes 8388608 | tf_op jit(solution)/shard_map/all_to_all | solution.py:97
  100.3 3.3 %sort_prefixfusion = f32[16,32]{1,0:T(8,128)S(1)} fusion(f32[16,512]{1,0:T(8,128)S(1)} %neg.18), kind=kCustom, calls=%sort.31.sort_prefix | custom fusion | flops 106496 | bytes 34816 | tf_op jit(solution)/shard_map/jit(sort)/sort | solution.py:15
  104.3 46.9 %all-to-all-done.4 = bf16[128,5,2048]{2,1,0:T(8,128)(2,1)} async-done(((bf16[128,5,2048]{2,1,0:T(8,128)(2,1)}), bf16[128,5,2048]{2,1,0:T(8,128)(2,1)}, u32[]{:S(2)}, u32[]{:S(2)}) %all-to-all-start.4) | async-done | bytes 2621472 | tf_op jit(solution)/shard_map/all_to_all | solution.py:97
  151.2 4.2 %reshape.242 = bf16[640,2048]{1,0:T(8,128)(2,1)S(1)} reshape(bf16[128,5,2048]{2,1,0:T(8,128)(2,1)} %all-to-all-done.4) | data formatting | bytes 5242880 | tf_op jit(solution)/shard_map/reshape | solution.py:98
  155.4 3.3 %gather_fusion.2 = bf16[512,2048]{1,0:T(8,128)(2,1)} fusion(bf16[640,2048]{1,0:T(8,128)(2,1)S(1)} %reshape.242, s32[1024]{0:T(1024)S(1)} %pad_clamp_fusion), kind=kCustom, calls=%fused_computation.2 | custom fusion | bytes 4196352 | tf_op jit(solution)/shard_map/gather | solution.py:98
  158.8 2.8 %fusion.6 = f32[16,1,32]{2,1,0:T(1,128)} fusion(bf16[16,32,2048]{2,1,0:T(8,128)(2,1)} %bitcast.38, bf16[16,2048,1]{1,0,2:T(8,128)(2,1)S(1)} %fusion.12), kind=kOutput, calls=%fused_computation.25 | convolution fusion | flops 2097152 | bytes 2164736 | tf_op jit(solution)/shard_map/qsf,qf->qs/dot_general | solution.py:101
  (71 shorter events, 7.4 us)
Async XLA Ops:
  0.6 19.2 %copy-start.4 = (s32[16,32]{1,0:T(8,128)S(1)}, s32[16,32]{1,0:T(8,128)}, u32[]{:S(2)}) copy-start(s32[16,32]{1,0:T(8,128)} %param.14) | copy-start | bytes 6148
  0.6 19.2 %copy-start.3 = (s32[16,32]{1,0:T(8,128)S(1)}, s32[16,32]{1,0:T(8,128)}, u32[]{:S(2)}) copy-start(s32[16,32]{1,0:T(8,128)} %param.15) | copy-start | bytes 6148
  0.7 31.1 %copy-start.5 = (s32[16]{0:T(128)S(1)}, s32[16]{0:T(128)}, u32[]{:S(2)}) copy-start(s32[16]{0:T(128)} %param.12) | copy-start | bytes 196
  4.6 20.9 %all-to-all-start = ((bf16[128,1,2]{2,1,0:T(2,128)(2,1)}), bf16[128,1,2]{2,1,0:T(2,128)(2,1)S(1)}, u32[]{:S(2)}, u32[]{:S(2)}) async-start(bf16[128,1,2]{2,1,0:T(2,128)(2,1)} %convert_element_type.58), calls=%async_computation | async-start | bytes 131072 | tf_op jit(solution)/shard_map/all_to_all | solution.py:66
  25.5 15.3 %all-to-all-start.3 = ((s32[128,1,5]{2,1,0:T(1,128)}), s32[128,1,5]{2,1,0:T(1,128)S(1)}, u32[]{:S(2)}, u32[]{:S(2)}) async-start(s32[128,1,5]{2,1,0:T(1,128)} %bitcast.12), calls=%async_computation.3 | async-start | bytes 131072 | tf_op jit(solution)/shard_map/all_to_all | solution.py:95
  40.8 14.5 %all-to-all-start.1 = ((bf16[128,2,256]{2,1,0:T(2,128)(2,1)}), bf16[128,2,256]{2,1,0:T(2,128)(2,1)S(1)}, u32[]{:S(2)}, u32[]{:S(2)}) async-start(bf16[128,2,256]{2,1,0:T(2,128)(2,1)} %reshape.235), calls=%async_computation.1 | async-start | bytes 262144 | tf_op jit(solution)/shard_map/all_to_all | solution.py:65
  67.2 21.5 %all-to-all-start.2 = ((f32[128,2,32]{2,1,0:T(2,128)}), f32[128,2,32]{2,1,0:T(2,128)S(1)}, u32[]{:S(2)}, u32[]{:S(2)}) async-start(f32[128,2,32]{2,1,0:T(2,128)} %bitcast.4), calls=%async_computation.2 | async-start | bytes 262144 | tf_op jit(solution)/shard_map/all_to_all | solution.py:79
  88.6 10.4 %copy-start.2 = (s32[16,16]{1,0:T(8,128)S(1)}, s32[16,16]{1,0:T(8,128)}, u32[]{:S(2)}) copy-start(s32[16,16]{1,0:T(8,128)} %param.9) | copy-start | bytes 3076
  88.7 10.5 %copy-start.1 = (s32[16,32]{1,0:T(8,128)S(1)}, s32[16,32]{1,0:T(8,128)}, u32[]{:S(2)}) copy-start(s32[16,32]{1,0:T(8,128)} %param.13) | copy-start | bytes 6148
  88.7 10.6 %copy-start = (bf16[16,2048]{1,0:T(8,128)(2,1)S(1)}, bf16[16,2048]{1,0:T(8,128)(2,1)}, u32[]{:S(2)}) copy-start(bf16[16,2048]{1,0:T(8,128)(2,1)} %param.8) | copy-start | bytes 196612
  88.7 62.6 %all-to-all-start.4 = ((bf16[128,5,2048]{2,1,0:T(8,128)(2,1)}), bf16[128,5,2048]{2,1,0:T(8,128)(2,1)}, u32[]{:S(2)}, u32[]{:S(2)}) async-start(bf16[128,5,2048]{2,1,0:T(8,128)(2,1)} %reshape.254), calls=%async_computation.4 | async-start | bytes 8388608 | tf_op jit(solution)/shard_map/all_to_all | solution.py:97
where the time goes:
time: 162 us
  waiting for transfers between devices  69.6 us (43%)
  starting transfers between devices  36.6 us (23%)
  local copies, waits for them, and re-layouts  32.9 us (20%)
  other arithmetic  16.2 us (10%)
  matrix products  5.39 us (3%)
    all_to_all x1, waiting for transfers between devices, shards(): lax.all_to_all(found_rows, ('gx', 'gy'), split_axis=0, concat_axis=0, til...  46.9 us
    gather x2, local copies, waits for them, and re-layouts, shards(): doc_table[lax.all_to_all(requests, ('gx', 'gy'), split_axis=0, concat_axi...  17.1 us
    sort x2, other arithmetic, top_values(): return -jnp.sort(-values, axis=-1)[..., :count]  11.8 us
    all_to_all x1, starting transfers between devices, shards(): lax.all_to_all(send_list, ('gx', 'gy'), split_axis=0, concat_axis=0, tile...  11.5 us
    all_to_all x1, starting transfers between devices, shards(): lax.all_to_all(found_rows, ('gx', 'gy'), split_axis=0, concat_axis=0, til...  10.3 us
    all_to_all x1, waiting for transfers between devices, shards(): lax.all_to_all(send_prefix, ('gx', 'gy'), split_axis=0, concat_axis=0, ti...  9.73 us
    all_to_all x1, waiting for transfers between devices, shards(): lax.all_to_all(requests, ('gx', 'gy'), split_axis=0, concat_axis=0, tiled...  8.97 us
    all_to_all x1, starting transfers between devices, shards(): lax.all_to_all(requests, ('gx', 'gy'), split_axis=0, concat_axis=0, tiled...  5.85 us
  transfers between devices with their start and end apart: 5, of which 4 were waited for; matrix products, arithmetic and copies ran while one was open for 17% of the time, Pallas kernels for 0%

commit v1 on v0

v1 whole, which is shorter than its diff:
```python
import jax
import jax.numpy as jnp
from jax import lax
from jax.experimental import pallas as pl
from jax.experimental.pallas import tpu as pltpu
from jax.sharding import PartitionSpec as P

MESH = pl.DeviceIdType.MESH
SIDE = 4
DEVS = 128
QROWS = 16
LISTS = 16
ROWS = 256
ELIG = 96
PREFIX = 256
FULL = 2048
TILES = FULL // 128
CAP = 5
PCAP = 2
TOPK = 32
SHORT = 32
PROBES = 16
LOW = -1e30
PARTS = ((0, 6), (6, 11), (11, 16))
F32 = jnp.float32
BF16 = jnp.bfloat16
I32 = jnp.int32
LANE_CODE, LANE_ROW, LANE_LIST, LANE_PROW = 0, 8, 16, 24


def iota(shape, axis):
    return lax.broadcasted_iota(I32, shape, axis)


def merge_down(seq):
    seq = list(seq)
    step = len(seq) // 2
    while step:
        for i in range(len(seq)):
            if not i & step:
                a, b = seq[i], seq[i + step]
                seq[i], seq[i + step] = jnp.maximum(a, b), jnp.minimum(a, b)
        step //= 2
    return seq


def sort_down(seq):
    if len(seq) == 1:
        return list(seq)
    half = len(seq) // 2
    return merge_down(sort_down(seq[:half]) + sort_down(seq[half:])[::-1])


def join_rolled(seq, shift, axis):
    count = len(seq)
    other = [pltpu.roll(v, shift, axis) for v in seq]
    return merge_down([jnp.maximum(seq[i], other[count - 1 - i]) for i in range(count)])


def coords():
    gx, gy = lax.axis_index("gx"), lax.axis_index("gy")
    return gx // SIDE, gx % SIDE, gy // 2, gy % 2


def device_of(y, x, z, c):
    return (y * SIDE + x, z * 2 + c)


def at_offset(me, off):
    y = (me[0] + off // 32) % SIDE
    x = (me[1] + off // 8 % SIDE) % SIDE
    z = (me[2] + off // 2 % SIDE) % SIDE
    c = (me[3] + off % 2) % 2
    return device_of(y, x, z, c), (y * SIDE + x) * 8 + z * 2 + c


def back_offset(off):
    y = (SIDE - off // 32) % SIDE
    x = (SIDE - off // 8 % SIDE) % SIDE
    z = (SIDE - off // 2 % SIDE) % SIDE
    return (y * SIDE + x) * 8 + z * 2 + off % 2


class Gather:
    def __init__(self, qbuf, send_sem, recv_sem, me):
        self.qbuf, self.send_sem, self.recv_sem, self.me = qbuf, send_sem, recv_sem, me
        self.count = 0
        self.copies = []

    def view(self, where, tiles, core=0):
        return self.qbuf.at[where[0], where[1], where[2], core, tiles]

    def start(self, src, dst, peer):
        number = self.count
        self.count += 1
        copy = pltpu.make_async_remote_copy(
            src_ref=src,
            dst_ref=dst,
            send_sem=self.send_sem.at[number],
            recv_sem=self.recv_sem.at[number],
            device_id=peer,
            device_id_type=MESH,
        )
        copy.start()
        self.copies.append(copy)
        return copy

    def peer(self, axis, step):
        place = list(self.me)
        place[axis] = (place[axis] + SIDE + step) % SIDE
        return device_of(*place)

    def partner(self):
        y, x, z, c = self.me
        return device_of(y, x, z, 1 - c)

    def set_axis(self, unit, axis, value):
        where = list(unit)
        where[axis] = value
        return where

    def ring_start(self, unit, axis, tiles):
        own = self.view(self.set_axis(unit, axis, 0), tiles)
        fwd = self.start(own, self.view(self.set_axis(unit, axis, 3), tiles), self.peer(axis, 1))
        bwd = self.start(own, self.view(self.set_axis(unit, axis, 1), tiles), self.peer(axis, -1))
        middle = (tiles.start + tiles.stop + axis % 2) // 2
        halves = (slice(tiles.start, middle), slice(middle, tiles.stop))
        return dict(unit=unit, axis=axis, tiles=tiles, fwd=fwd, bwd=bwd, halves=halves)

    def ring_low(self, ring):
        ring["fwd"].wait_recv()
        unit, axis, tiles = ring["unit"], ring["axis"], ring["halves"][0]
        ring["end_fwd"] = self.start(
            self.view(self.set_axis(unit, axis, 3), tiles),
            self.view(self.set_axis(unit, axis, 2), tiles),
            self.peer(axis, 1),
        )

    def ring_high(self, ring):
        ring["bwd"].wait_recv()
        unit, axis, tiles = ring["unit"], ring["axis"], ring["halves"][1]
        ring["end_bwd"] = self.start(
            self.view(self.set_axis(unit, axis, 1), tiles),
            self.view(self.set_axis(unit, axis, 2), tiles),
            self.peer(axis, -1),
        )

    def ring_end(self, ring):
        ring["end_fwd"].wait_recv()
        ring["end_bwd"].wait_recv()

    def across(self, where, tiles):
        return self.start(self.view(where, tiles, 0), self.view(where, tiles, 1), self.partner())

    def run(self):
        every = slice(0, SIDE)
        rest = slice(1, SIDE)
        parts = []
        for number, (low, high) in enumerate(PARTS):
            axes = (number, (number + 1) % 3, (number + 2) % 3)
            parts.append(dict(axes=axes, tiles=slice(low, high)))

        def unit(axes, a, b, c):
            where = [0, 0, 0]
            where[axes[0]], where[axes[1]], where[axes[2]] = a, b, c
            return where

        partner = [self.across([0, 0, 0], slice(0, TILES))]
        for part in parts:
            a, b, c = part["axes"]
            part["A"] = self.ring_start([0, 0, 0], a, part["tiles"])
        for part in parts:
            a, b, c = part["axes"]
            part["B0"] = self.ring_start([0, 0, 0], b, part["tiles"])
            part["C0"] = self.ring_start([0, 0, 0], c, part["tiles"])
        for part in parts:
            self.ring_low(part["A"])
            self.ring_high(part["A"])
        for part in parts:
            for name in ("B0", "C0"):
                self.ring_low(part[name])
                self.ring_high(part[name])
        for part in parts:
            axes, tiles = part["axes"], part["tiles"]
            self.ring_end(part["A"])
            part["B1"] = self.ring_start(unit(axes, rest, 0, 0), axes[1], tiles)
            part["C1"] = self.ring_start(unit(axes, rest, 0, 0), axes[2], tiles)
            partner.append(self.across(unit(axes, rest, 0, 0), tiles))
        for part in parts:
            axes, tiles = part["axes"], part["tiles"]
            self.ring_low(part["B1"])
            part["C2"] = self.ring_start(unit(axes, every, 3, 0), axes[2], tiles)
            partner.append(self.across(unit(axes, every, 3, 0), tiles))
            self.ring_high(part["B1"])
            part["C3"] = self.ring_start(unit(axes, every, 1, 0), axes[2], tiles)
            partner.append(self.across(unit(axes, every, 1, 0), tiles))
        for part in parts:
            self.ring_low(part["C1"])
            self.ring_high(part["C1"])
        for part in parts:
            axes, tiles = part["axes"], part["tiles"]
            self.ring_end(part["B0"])
            self.ring_end(part["B1"])
            part["C4"] = self.ring_start(unit(axes, every, 2, 0), axes[2], tiles)
            partner.append(self.across(unit(axes, every, 2, 0), tiles))
        for part in parts:
            axes, tiles = part["axes"], part["tiles"]
            self.ring_end(part["C0"])
            partner.append(self.across(unit(axes, 0, 0, rest), tiles))
            self.ring_end(part["C1"])
            partner.append(self.across(unit(axes, rest, 0, rest), tiles))
        for name, b in (("C2", 3), ("C3", 1), ("C4", 2)):
            for part in parts:
                axes, tiles = part["axes"], part["tiles"]
                self.ring_low(part[name])
                partner.append(self.across(unit(axes, every, b, 3), tiles))
                self.ring_high(part[name])
                partner.append(self.across(unit(axes, every, b, 1), tiles))
        for name, b in (("C2", 3), ("C3", 1), ("C4", 2)):
            for part in parts:
                axes, tiles = part["axes"], part["tiles"]
                self.ring_end(part[name])
                partner.append(self.across(unit(axes, every, b, 2), tiles))
        for copy in partner:
            copy.wait_recv()
        for copy in self.copies:
            copy.wait_send()


def kernel(
    q_hbm, docs_hbm, lengths, sdev_ref, slist_ref, srow_ref, pdev_ref, plist_ref,
    ptop_ref, resc_ref,
    qbuf, docs, dpre, gath, oh, psel, sel, tabsend, tabrecv, psend, precv, rsend, rrecv,
    load_sem, gsend, grecv, xsend, xrecv,
):
    me = coords()
    own_number = (me[0] * SIDE + me[1]) * 8 + me[2] * 2 + me[3]

    for t in range(TILES):
        pltpu.make_async_copy(
            q_hbm.at[:, pl.ds(t * 128, 128)], qbuf.at[0, 0, 0, 0, t], load_sem.at[0]
        ).start()
    docs_copy = pltpu.make_async_copy(docs_hbm.at[:, pl.ds(0, ELIG), :], docs, load_sem.at[1])
    docs_copy.start()
    dpre_copy = pltpu.make_async_copy(docs_hbm.at[:, :, pl.ds(0, PREFIX)], dpre, load_sem.at[2])
    dpre_copy.start()

    barrier = pltpu.get_barrier_semaphore()

    def greet(off, carry):
        peer, _ = at_offset(me, off)
        pl.semaphore_signal(barrier, inc=1, device_id=peer, device_id_type=MESH)
        return carry

    lax.fori_loop(1, DEVS, greet, 0)

    dev = iota((QROWS, DEVS), 1)
    sdev = sdev_ref[...]
    scode = (slist_ref[...] * ELIG + srow_ref[...] + 1).astype(F32)
    pdev = pdev_ref[...]
    pcode = (plist_ref[...] + 1).astype(F32)
    lower = (iota((QROWS, QROWS), 1) < iota((QROWS, QROWS), 0)).astype(F32).astype(BF16)
    qnum = iota((QROWS, DEVS), 0).astype(F32) + 1.0

    def table(devs, codes, width):
        got = jnp.zeros((QROWS, DEVS), F32)
        for s in range(width):
            got = got + jnp.where(devs[:, s : s + 1] == dev, codes[:, s : s + 1], 0.0)
        used = jnp.where(got > 0.0, 1.0, 0.0)
        rank = jnp.dot(lower, used.astype(BF16), preferred_element_type=F32)
        return got, jnp.where(used > 0.0, rank, -1.0)

    stab, srank = table(sdev, scode, SHORT)
    ptab, prank = table(pdev, pcode, PROBES)
    krow = iota((32, DEVS), 0)
    slots = jnp.zeros((32, DEVS), F32)
    for base, row_base, tab, rank, cap in (
        (LANE_CODE, LANE_ROW, stab, srank, CAP),
        (LANE_LIST, LANE_PROW, ptab, prank, PCAP),
    ):
        for j in range(cap):
            hit = rank == float(j)
            code = jnp.sum(jnp.where(hit, tab, 0.0), axis=0, keepdims=True) - 1.0
            row = jnp.sum(jnp.where(hit, qnum, 0.0), axis=0, keepdims=True) - 1.0
            slots = jnp.where(krow == base + j, code, slots)
            slots = jnp.where(krow == row_base + j, row, slots)
    slots = jnp.concatenate([slots, jnp.zeros((96, DEVS), F32)], axis=0)
    tabsend[...] = slots.T.astype(I32).reshape(DEVS, 1, DEVS)

    pltpu.make_async_copy(qbuf.at[0, 0, 0, 1], qbuf.at[0, 0, 0, 0], load_sem.at[0]).wait()
    pl.semaphore_wait(barrier, DEVS - 1)

    def exchange(send, recv, number, by_offset):
        def body(off, carry):
            peer, flat = at_offset(me, off)
            if by_offset:
                src, dst = send.at[off], recv.at[own_number]
            else:
                src, dst = send.at[flat], recv.at[back_offset(off)]
            pltpu.make_async_remote_copy(
                src_ref=src, dst_ref=dst, send_sem=xsend.at[number], recv_sem=xrecv.at[number],
                device_id=peer, device_id_type=MESH,
            ).start()
            return carry

        lax.fori_loop(1, DEVS, body, 0)

    def exchanged(send, recv, number):
        rest = pl.ds(0, DEVS - 1)
        pltpu.make_async_copy(recv.at[rest], recv.at[rest], xrecv.at[number]).wait()
        pltpu.make_async_copy(send.at[rest], send.at[rest], xsend.at[number]).wait()

    exchange(tabsend, tabrecv, 0, False)
    gather = Gather(qbuf, gsend, grecv, me)
    gather.run()
    exchanged(tabsend, tabrecv, 0)
    tabrecv[0] = tabsend[own_number]
    docs_copy.wait()
    dpre_copy.wait()

    slot = tabrecv[...].reshape(DEVS, DEVS)
    slot_t = slot.astype(F32).T

    doc_number = iota((DEVS, LISTS * ELIG), 1)
    for j in range(CAP):
        hit = slot[:, LANE_CODE + j : LANE_CODE + j + 1] == doc_number
        oh[pl.ds(j * DEVS, DEVS), :] = jnp.where(hit, 1.0, 0.0).astype(BF16)

    def pick(n, carry):
        cols = pl.ds(pl.multiple_of(n * 256, 256), 256)
        block = docs[:, :, cols].reshape(LISTS * ELIG, 256)
        got = jnp.dot(oh[...], block, preferred_element_type=F32)
        gath[:, :, cols] = got.astype(BF16).reshape(CAP, DEVS, 256)
        return carry

    lax.fori_loop(0, FULL // 256, pick, 0)

    def queries(g, t):
        half = g % 2
        return qbuf[g // 2, pl.ds(half * 2, 2), :, :, t].reshape(256, 128)

    group_row = iota((16, 1), 0)
    group_col = iota((16, 256), 1)

    def own_column(rows, lane):
        number = rows[:, lane : lane + 1]
        return jnp.where(number < 0, -1, group_row * QROWS + number)

    def prefixes(g, carry):
        here = pl.ds(pl.multiple_of(g * 16, 16), 16)
        rows = tabrecv[here].reshape(16, DEVS)
        hits = [
            jnp.where(own_column(rows, LANE_PROW + p) == group_col, 1.0, 0.0) for p in range(PCAP)
        ]
        hit = jnp.concatenate(hits, axis=0).astype(BF16)
        for t in range(PREFIX // 128):
            got = jnp.dot(hit, queries(g, t), preferred_element_type=F32).astype(BF16)
            psel[:, here, pl.ds(t * 128, 128)] = got.reshape(PCAP, 16, 128)
        return carry

    lax.fori_loop(0, 8, prefixes, 0)

    lists = jnp.concatenate([slot_t[LANE_LIST + p : LANE_LIST + p + 1, :] for p in range(PCAP)], axis=1)
    wanted = psel[...].reshape(PCAP * DEVS, PREFIX)
    rows_valid = jnp.zeros((1, PCAP * DEVS), I32)
    for n in range(LISTS):
        rows_valid = jnp.where(lists == float(n), lengths[n], rows_valid)

    def score(n, carry):
        got = lax.dot_general(
            dpre[n], wanted, (((1,), (1,)), ((), ())), preferred_element_type=F32
        )
        sel[...] = jnp.where(lists == n.astype(F32), got, sel[...])
        return carry

    sel[...] = jnp.zeros_like(sel)
    lax.fori_loop(0, LISTS, score, 0)

    sub = iota((8, DEVS), 0)
    tops = []
    for p in range(PCAP):
        lanes = pl.ds(p * DEVS, DEVS)
        bound = rows_valid[:, p * DEVS : (p + 1) * DEVS]
        seq = [
            jnp.where(sub + v * 8 < bound, sel[pl.ds(v * 8, 8), lanes], LOW) for v in range(32)
        ]
        seq = sort_down(seq)
        for shift in (4, 2, 1):
            seq = join_rolled(seq, shift, 0)
        for m in range(TOPK // 8):
            block = seq[m * 8]
            for s in range(1, 8):
                block = jnp.where(sub == s, seq[m * 8 + s], block)
            tops.append(block)
    tops.append(jnp.zeros((DEVS - PCAP * TOPK, DEVS), F32))
    psend[...] = jnp.concatenate(tops, axis=0).T.reshape(DEVS, 1, DEVS)
    exchange(psend, precv, 1, True)

    lane = iota((16, DEVS), 1)

    def rescore(g, carry):
        here = pl.ds(pl.multiple_of(g * 16, 16), 16)
        rows = tabrecv[here].reshape(16, DEVS)
        got = jnp.zeros((CAP * 16, 256), F32)
        for k in range(FULL // 256):
            left = gath[:, here, pl.ds(k * 256, 256)].reshape(CAP * 16, 256)
            right = jnp.concatenate([queries(g, 2 * k), queries(g, 2 * k + 1)], axis=1)
            got = got + lax.dot_general(
                left, right, (((1,), (1,)), ((), ())), preferred_element_type=F32
            )
        out = jnp.zeros((16, DEVS), F32)
        for j in range(CAP):
            hit = own_column(rows, LANE_ROW + j) == group_col
            value = jnp.sum(
                jnp.where(hit, got[j * 16 : (j + 1) * 16, :], 0.0), axis=1, keepdims=True
            )
            out = jnp.where(lane == j, value, out)
        rsend[here] = out.reshape(16, 1, DEVS)
        return carry

    lax.fori_loop(0, 8, rescore, 0)
    exchange(rsend, rrecv, 2, True)

    squares = jnp.zeros((QROWS, 128), F32)
    for t in range(TILES):
        value = qbuf[0, 0, 0, 0, t].astype(F32)
        squares = squares + value * value
        if t == PREFIX // 128 - 1:
            prefix_squares = squares
    full_scale = 1.0 / jnp.sqrt(1.0 + jnp.sum(squares, axis=1, keepdims=True))
    prefix_scale = 1.0 / jnp.sqrt(1.0 + jnp.sum(prefix_squares, axis=1, keepdims=True))

    exchanged(psend, precv, 1)
    precv[own_number] = psend[0]
    back = precv[...].reshape(DEVS, DEVS).T
    first, second = prank == 0.0, prank == 1.0
    seq = [
        jnp.where(first, back[k : k + 1, :], jnp.where(second, back[TOPK + k : TOPK + k + 1, :], LOW))
        for k in range(TOPK)
    ]
    for shift in (64, 32, 16, 8, 4, 2, 1):
        seq = join_rolled(seq, shift, 1)
    best = seq[0]
    for k in range(1, TOPK):
        best = jnp.where(lane == k, seq[k], best)
    ptop_ref[...] = (best * prefix_scale)[:, :TOPK]

    exchanged(rsend, rrecv, 2)
    rrecv[own_number] = rsend[0]
    back = rrecv[...].reshape(DEVS, DEVS).T
    value = jnp.zeros((QROWS, DEVS), F32)
    for j in range(CAP):
        value = jnp.where(srank == float(j), back[j : j + 1, :], value)
    out = jnp.zeros((QROWS, DEVS), F32)
    for s in range(SHORT):
        one = jnp.sum(
            jnp.where(sdev[:, s : s + 1] == dev, value, 0.0), axis=1, keepdims=True
        )
        out = jnp.where(lane == s, one, out)
    resc_ref[...] = (out * full_scale)[:, :SHORT]


COPIES = 3 * 32 + 1 + 3 * 15


def shards(queries, probe_dev, probe_list, documents, lengths, short_dev, short_list, short_row):
    vmem = pl.BlockSpec(memory_space=pltpu.VMEM)
    anywhere = pl.BlockSpec(memory_space=pl.ANY)
    row = (DEVS, 1, DEVS)
    return pl.pallas_call(
        kernel,
        name="search",
        out_shape=(
            jax.ShapeDtypeStruct((QROWS, TOPK), F32),
            jax.ShapeDtypeStruct((QROWS, SHORT), F32),
        ),
        in_specs=[anywhere, anywhere, pl.BlockSpec(memory_space=pltpu.SMEM)] + [vmem] * 5,
        out_specs=(vmem, vmem),
        scratch_shapes=[
            pltpu.VMEM((SIDE, SIDE, SIDE, 2, TILES, QROWS, 128), BF16),
            pltpu.VMEM((LISTS, ELIG, FULL), BF16),
            pltpu.VMEM((LISTS, ROWS, PREFIX), BF16),
            pltpu.VMEM((CAP, DEVS, FULL), BF16),
            pltpu.VMEM((CAP * DEVS, LISTS * ELIG), BF16),
            pltpu.VMEM((PCAP, DEVS, PREFIX), BF16),
            pltpu.VMEM((ROWS, PCAP * DEVS), F32),
            pltpu.VMEM(row, I32),
            pltpu.VMEM(row, I32),
            pltpu.VMEM(row, F32),
            pltpu.VMEM(row, F32),
            pltpu.VMEM(row, F32),
            pltpu.VMEM(row, F32),
            pltpu.SemaphoreType.DMA((3,)),
            pltpu.SemaphoreType.DMA((COPIES,)),
            pltpu.SemaphoreType.DMA((COPIES,)),
            pltpu.SemaphoreType.DMA((3,)),
            pltpu.SemaphoreType.DMA((3,)),
        ],
        compiler_params=pltpu.CompilerParams(
            collective_id=0, has_side_effects=True, vmem_limit_bytes=60 * 1024 * 1024
        ),
    )(queries, documents, lengths, short_dev, short_list, short_row, probe_dev, probe_list)


def solution(mesh):
    spread = P(("gx", "gy"), None)
    in_specs = (spread, spread, spread, P(("gx", "gy"), None, None), P(("gx", "gy")), spread, spread, spread)
    return jax.shard_map(shards, mesh=mesh, in_specs=in_specs, out_specs=(spread, spread), check_vma=False)
```

time: 162 us -> 83.9 us (0.52)
  Pallas kernels: 0 us -> 80.4 us
  waiting for transfers between devices: 69.6 us -> 0 us
  starting transfers between devices: 36.6 us -> 0 us
  local copies, waits for them, and re-layouts: 32.9 us -> 2.59 us
  other arithmetic: 16.2 us -> 0 us
  matrix products: 5.39 us -> 0 us
    pallas_call x0 -> x1, Pallas kernels: none -> 80.4 us  [shards(): pl.pallas_call(kernel, name='search', out_shape=(jax.ShapeDtypeStruct((QR...]
    all_to_all x5 -> x0, waiting for transfers between devices: 69.6 us -> none  [the longest x1 46.9 us: shards(): lax.all_to_all(found_rows, ('gx', 'gy'), split_axis=0, concat_axis=0, til...]
    all_to_all x5 -> x0, starting transfers between devices: 36.6 us -> none  [the longest x1 11.5 us: shards(): lax.all_to_all(send_list, ('gx', 'gy'), split_axis=0, concat_axis=0, tile...]
    gather x4 -> x0, local copies, waits for them, and re-layouts: 21.2 us -> none  [the longest x2 17.1 us: shards(): doc_table[lax.all_to_all(requests, ('gx', 'gy'), split_axis=0, concat_axi...]
    sort x2 -> x0, other arithmetic: 11.8 us -> none  [top_values(): return -jnp.sort(-values, axis=-1)[..., :count]]
    reshape x5 -> x0, local copies, waits for them, and re-layouts: 6.48 us -> none  [the longest x1 4.18 us: shards(): fetched.reshape(count_dev * capacity, -1)[flat_slots]]
    dot_general x3 -> x0, matrix products: 5.39 us -> none  [the longest x1 2.84 us: shards(): jnp.einsum('qsf,qf->qs', vectors, full_unit, preferred_element_type=jnp.f...]
    unnamed x13 -> x2, local copies, waits for them, and re-layouts: 0.15 us -> 2.59 us
  transfers between devices with their start and end apart: 5 -> 0, of which waited for: 4 -> 0; matrix products, arithmetic and copies ran while one was open for 17% -> 0% of each run, Pallas kernels for 0% -> 0%
where the time goes in v1:
time: 83.9 us; the launch traced here: 83.7 us
  Pallas kernels  80.4 us (96%)
  local copies, waits for them, and re-layouts  2.59 us (3%)
    pallas_call x1, Pallas kernels, shards(): pl.pallas_call(kernel, name='search', out_shape=(jax.ShapeDtypeStruct((QR...  80.4 us
    unnamed x2, local copies, waits for them, and re-layouts  2.59 us

profile of v1, /device:TPU:1, one launch (start us, length us, event | category | flops | bytes accessed | tf_op | source)
XLA Modules:
  0.0 83.7 jit_solution(3341017326292420314)
XLA Ops:
  0.6 80.4 %search.1 = (f32[16,32]{1,0:T(8,128)}, f32[16,32]{1,0:T(8,128)}) custom-call(bf16[16,2048]{1,0:T(8,128)(2,1)} %q_hbm.1, bf16[16,256,2048]{2,1,0:T(8,128)(2,1)} %docs_hbm.1, s32[16]{0:T(128)} %lengths.1, s32[16,32]{1,0:T(8,128)} %sdev_ref.1, s32[16,32]{1,0:T(8,128)} %slist_ref.1, s32[16,32]{1,0:T(8,128)} %srow_ref.1, s32[16,16]{1,0:T(8,128)} %pdev_ref.1, ...), custom_call_target="tpu_custom_call" | custom-call | tf_op jit(solution)/shard_map/search/pallas_call | solution.py:470
  81.1 1.3 %copy.12 = f32[16,32]{1,0:T(8,128)} copy(f32[16,32]{1,0:T(8,128)} %get-tuple-element.4) | data formatting | bytes 4096
  82.4 1.3 %copy.13 = f32[16,32]{1,0:T(8,128)} copy(f32[16,32]{1,0:T(8,128)} %get-tuple-element.5) | data formatting | bytes 4096

commit v2 on v1

v2 whole, which is shorter than its diff:
```python
import jax
import jax.numpy as jnp
from jax import lax
from jax.experimental import pallas as pl
from jax.experimental.pallas import tpu as pltpu
from jax.sharding import PartitionSpec as P

MESH = pl.DeviceIdType.MESH
SIDE = 4
DEVS = 128
QROWS = 16
LISTS = 16
ROWS = 256
ELIG = 96
PREFIX = 256
FULL = 2048
TILES = FULL // 128
CAP = 5
PCAP = 2
TOPK = 32
SHORT = 32
PROBES = 16
LOW = -1e30
PARTS = ((0, 6), (6, 12), (12, 16))
F32 = jnp.float32
BF16 = jnp.bfloat16
I32 = jnp.int32
LANE_CODE, LANE_ROW, LANE_LIST = 0, 5, 10
RINGS = 8


def iota(shape, axis):
    return lax.broadcasted_iota(I32, shape, axis)


def merge_down(seq):
    seq = list(seq)
    step = len(seq) // 2
    while step:
        for i in range(len(seq)):
            if not i & step:
                a, b = seq[i], seq[i + step]
                seq[i], seq[i + step] = jnp.maximum(a, b), jnp.minimum(a, b)
        step //= 2
    return seq


def sort_down(seq):
    if len(seq) == 1:
        return list(seq)
    half = len(seq) // 2
    return merge_down(sort_down(seq[:half]) + sort_down(seq[half:])[::-1])


def join_rolled(seq, shift, axis):
    count = len(seq)
    other = [pltpu.roll(v, shift, axis) for v in seq]
    return merge_down([jnp.maximum(seq[i], other[count - 1 - i]) for i in range(count)])


def coords():
    gx, gy = lax.axis_index("gx"), lax.axis_index("gy")
    return gx // SIDE, gx % SIDE, gy // 2, gy % 2


def device_of(y, x, z, c):
    return (y * SIDE + x, z * 2 + c)


def for_peers(me, visit):
    steps = range(SIDE)
    xs = [(me[1] + d) % SIDE for d in steps]
    zs = [(me[2] + d) % SIDE * 2 for d in steps]
    gys = [[z + me[3], z + 1 - me[3]] for z in zs]

    def visit_one(dy, back_dy, gx, dx, dz, dc):
        gy = gys[dz][dc]
        off = dy * 32 + (dx * 8 + dz * 2 + dc)
        back = back_dy * 32 + ((SIDE - dx) % SIDE * 8 + (SIDE - dz) % SIDE * 2 + dc)
        visit((gx, gy), gx * 8 + gy, off, back)

    def plane(dy, carry):
        back_dy = (SIDE - dy) % SIDE
        row = (me[0] + dy) % SIDE * SIDE
        for dx in steps:
            gx = row + xs[dx]
            for dz in steps:
                for dc in range(2):
                    if dx or dz or dc:
                        visit_one(dy, back_dy, gx, dx, dz, dc)
        return carry

    for dy in range(1, SIDE):
        visit_one(dy, SIDE - dy, (me[0] + dy) % SIDE * SIDE + xs[0], 0, 0, 0)
    lax.fori_loop(0, SIDE, plane, 0)


class Gather:
    def __init__(self, qbuf, send_sem, recv_sem, cross_sem, me):
        self.qbuf, self.send_sem, self.recv_sem = qbuf, send_sem, recv_sem
        self.cross_sem, self.me = cross_sem, me
        self.count = 0
        y, x, z, c = me
        self.partner = device_of(y, x, z, 1 - c)
        self.peers = {}
        for axis in range(3):
            for step in (1, 2, 3):
                place = list(me)
                place[axis] = (place[axis] + step) % SIDE
                self.peers[axis, step] = device_of(*place)

    def view(self, where, tiles, core=0):
        return self.qbuf.at[where[0], where[1], where[2], core, tiles]

    def next_sem(self):
        self.count += 1
        return self.recv_sem.at[self.count - 1]

    def start(self, src, dst, peer, sem):
        copy = pltpu.make_async_remote_copy(
            src_ref=src, dst_ref=dst, send_sem=self.send_sem, recv_sem=sem,
            device_id=peer, device_id_type=MESH,
        )
        copy.start()
        return copy

    def slot(self, ring, value, tiles):
        where = list(ring["unit"])
        where[ring["axis"]] = value
        return self.view(where, tiles)

    def ring_start(self, unit, axis, tiles, far=False):
        ring = dict(unit=unit, axis=axis, tiles=tiles, end=self.next_sem())
        own = self.slot(ring, 0, tiles)
        ring["fwd"] = self.start(own, self.slot(ring, 3, tiles), self.peers[axis, 1], self.next_sem())
        ring["bwd"] = self.start(own, self.slot(ring, 1, tiles), self.peers[axis, 3], self.next_sem())
        if far:
            self.start(own, self.slot(ring, 2, tiles), self.peers[axis, 2], ring["end"])
        return ring

    def ring_low(self, ring, relay=True):
        ring["fwd"].wait_recv()
        if relay:
            tiles = slice(ring["tiles"].start, (ring["tiles"].start + ring["tiles"].stop) // 2)
            src, dst = self.slot(ring, 3, tiles), self.slot(ring, 2, tiles)
            self.start(src, dst, self.peers[ring["axis"], 1], ring["end"])

    def ring_high(self, ring, relay=True):
        ring["bwd"].wait_recv()
        if relay:
            tiles = slice((ring["tiles"].start + ring["tiles"].stop) // 2, ring["tiles"].stop)
            src, dst = self.slot(ring, 1, tiles), self.slot(ring, 2, tiles)
            self.start(src, dst, self.peers[ring["axis"], 3], ring["end"])

    def ring_end(self, ring):
        far = self.slot(ring, 2, ring["tiles"])
        pltpu.make_async_copy(far, far, ring["end"]).wait()

    def across(self, where, tiles):
        self.start(self.view(where, tiles, 0), self.view(where, tiles, 1), self.partner, self.cross_sem)

    def begin(self):
        self.parts = []
        for number, (low, high) in enumerate(PARTS):
            axes = (number, (number + 1) % 3, (number + 2) % 3)
            self.parts.append(dict(axes=axes, tiles=slice(low, high)))
        home = [0, 0, 0]
        for part in self.parts:
            part["A"] = self.ring_start(home, part["axes"][0], part["tiles"], far=True)
        for part in self.parts:
            part["B0"] = self.ring_start(home, part["axes"][1], part["tiles"])
            part["C0"] = self.ring_start(home, part["axes"][2], part["tiles"])
        self.across(home, slice(0, TILES))

    def run(self, work):
        every = slice(0, SIDE)
        rest = slice(1, SIDE)
        parts = self.parts

        def unit(part, a, b, c):
            where = [0, 0, 0]
            for axis, value in zip(part["axes"], (a, b, c)):
                where[axis] = value
            return where

        def to_c(part, name, a, b):
            where = unit(part, a, b, 0)
            part[name] = self.ring_start(where, part["axes"][2], part["tiles"])
            self.across(where, part["tiles"])

        for part in parts:
            self.ring_low(part["A"], relay=False)
            self.ring_high(part["A"], relay=False)
        for part in parts:
            for name in ("B0", "C0"):
                self.ring_low(part[name])
                self.ring_high(part[name])
        for part in parts:
            self.ring_end(part["A"])
            part["B1"] = self.ring_start(unit(part, rest, 0, 0), part["axes"][1], part["tiles"])
            to_c(part, "C1", rest, 0)
        work(0)
        for part in parts:
            self.ring_low(part["B1"])
            self.ring_high(part["B1"])
            to_c(part, "C2", every, 3)
            to_c(part, "C3", every, 1)
        work(1)
        for part in parts:
            self.ring_low(part["C1"])
            self.ring_high(part["C1"])
        work(2)
        for part in parts:
            self.ring_end(part["B0"])
            self.ring_end(part["B1"])
            to_c(part, "C4", every, 2)
        work(3)
        for part in parts:
            self.ring_end(part["C0"])
            self.across(unit(part, 0, 0, rest), part["tiles"])
            self.ring_end(part["C1"])
            self.across(unit(part, rest, 0, rest), part["tiles"])
        work(4)
        for name, b in (("C2", 3), ("C3", 1)):
            for part in parts:
                self.ring_low(part[name])
                self.across(unit(part, every, b, 3), part["tiles"])
                self.ring_high(part[name])
                self.across(unit(part, every, b, 1), part["tiles"])
            work(5 if b == 3 else 6)
        for name, b in (("C4", 2),):
            for part in parts:
                self.ring_low(part[name])
                self.across(unit(part, every, b, 3), part["tiles"])
                self.ring_high(part[name])
                self.across(unit(part, every, b, 1), part["tiles"])
        work(7)
        for name, b in (("C2", 3), ("C3", 1), ("C4", 2)):
            for part in parts:
                self.ring_end(part[name])
                self.across(unit(part, every, b, 2), part["tiles"])
        work(8)
        half = self.qbuf.at[:, :, :, 1]
        pltpu.make_async_copy(half, half, self.cross_sem).wait()

    def drain(self):
        rest = slice(1, SIDE)
        for ref in (
            self.qbuf.at[rest], self.qbuf.at[0, rest], self.qbuf.at[0, 0, rest], self.qbuf.at[0, 0, 0, 1]
        ):
            pltpu.make_async_copy(ref, ref, self.send_sem).wait()


def kernel(
    q_hbm, docs_hbm, lengths, sdev_ref, slist_ref, srow_ref, pdev_ref, plist_ref,
    ptop_ref, resc_ref,
    qbuf, docs, dpre, gath, oh, sel, slot_ref, ask, asked, psend, precv, rsend, rrecv,
    load_sem, gsend, grecv, gcross, xsend, xrecv,
):
    me = coords()
    own_number = (me[0] * SIDE + me[1]) * 8 + me[2] * 2 + me[3]
    for t in range(TILES):
        pltpu.make_async_copy(
            q_hbm.at[:, pl.ds(t * 128, 128)], qbuf.at[0, 0, 0, 0, t], load_sem.at[0]
        ).start()
    barrier = pltpu.get_barrier_semaphore()

    def greet(peer, flat, off, back):
        pl.semaphore_signal(barrier, inc=1, device_id=peer, device_id_type=MESH)

    for_peers(me, greet)
    docs_copy = pltpu.make_async_copy(docs_hbm.at[:, pl.ds(0, ELIG), :], docs, load_sem.at[1])
    docs_copy.start()
    dpre_copy = pltpu.make_async_copy(docs_hbm.at[:, :, pl.ds(0, PREFIX)], dpre, load_sem.at[2])
    dpre_copy.start()

    dev = iota((QROWS, DEVS), 1)
    sdev = sdev_ref[...]
    scode = (slist_ref[...] * ELIG + srow_ref[...] + 1).astype(F32)
    pdev = pdev_ref[...]
    pcode = (plist_ref[...] + 1).astype(F32)
    lower = (iota((QROWS, QROWS), 1) < iota((QROWS, QROWS), 0)).astype(F32).astype(BF16)
    qnum = iota((QROWS, DEVS), 0).astype(F32) + 1.0

    def table(devs, codes, width):
        got = jnp.zeros((QROWS, DEVS), F32)
        for s in range(width):
            got = got + jnp.where(devs[:, s : s + 1] == dev, codes[:, s : s + 1], 0.0)
        used = jnp.where(got > 0.0, 1.0, 0.0)
        rank = jnp.dot(lower, used.astype(BF16), preferred_element_type=F32)
        return got, jnp.where(used > 0.0, rank, -1.0)

    stab, srank = table(sdev, scode, SHORT)
    ptab, prank = table(pdev, pcode, PROBES)
    krow = iota((16, DEVS), 0)
    slots = jnp.zeros((16, DEVS), F32)
    for base, row_base, tab, rank, cap in (
        (LANE_CODE, LANE_ROW, stab, srank, CAP),
        (LANE_LIST, None, ptab, prank, PCAP),
    ):
        for j in range(cap):
            hit = rank == float(j)
            code = jnp.sum(jnp.where(hit, tab, 0.0), axis=0, keepdims=True) - 1.0
            slots = jnp.where(krow == base + j, code, slots)
            if row_base is not None:
                row = jnp.sum(jnp.where(hit, qnum, 0.0), axis=0, keepdims=True) - 1.0
                slots = jnp.where(krow == row_base + j, row, slots)
    both = jnp.concatenate([slots, prank, jnp.zeros((96, DEVS), F32)], axis=0).T
    ask[:, :, pl.ds(PCAP * PREFIX, DEVS)] = both.reshape(DEVS, 1, DEVS)

    pltpu.make_async_copy(qbuf.at[0, 0, 0, 1], qbuf.at[0, 0, 0, 0], load_sem.at[0]).wait()
    squares = jnp.zeros((QROWS, 128), F32)
    for t in range(TILES):
        value = qbuf[0, 0, 0, 0, t].astype(F32)
        squares = squares + value * value
        if t == PREFIX // 128 - 1:
            prefix_squares = squares
    full_norm = jnp.sqrt(1.0 + jnp.sum(squares, axis=1, keepdims=True))
    prefix_norm = jnp.sqrt(1.0 + jnp.sum(prefix_squares, axis=1, keepdims=True))
    for p in range(PCAP):
        hit = jnp.where(both[:, 16:32] == float(p), 1.0, 0.0).astype(BF16)
        for t in range(PREFIX // 128):
            unit = (qbuf[0, 0, 0, 0, t].astype(F32) / prefix_norm).astype(BF16)
            rows = jnp.dot(hit, unit, preferred_element_type=F32)
            ask[:, :, pl.ds(p * PREFIX + t * 128, 128)] = rows.reshape(DEVS, 1, 128)

    pl.semaphore_wait(barrier, DEVS - 1)

    def exchange(send, recv, number, by_offset):
        def visit(peer, flat, off, back):
            if by_offset:
                src, dst = send.at[off], recv.at[own_number]
            else:
                src, dst = send.at[flat], recv.at[back]
            pltpu.make_async_remote_copy(
                src_ref=src, dst_ref=dst, send_sem=xsend.at[number], recv_sem=xrecv.at[number],
                device_id=peer, device_id_type=MESH,
            ).start()

        for_peers(me, visit)

    def exchanged(send, recv, number):
        rest = pl.ds(0, DEVS - 1)
        pltpu.make_async_copy(recv.at[rest], recv.at[rest], xrecv.at[number]).wait()
        pltpu.make_async_copy(send.at[rest], send.at[rest], xsend.at[number]).wait()

    gather = Gather(qbuf, gsend, grecv, gcross, me)
    gather.begin()
    exchange(ask, asked, 0, False)

    lane = iota((16, DEVS), 1)

    def read_slots():
        exchanged(ask, asked, 0)
        asked[0] = ask[own_number]
        docs_copy.wait()
        dpre_copy.wait()
        slot_ref[...] = asked[:, :, pl.ds(PCAP * PREFIX, DEVS)].reshape(DEVS, DEVS).astype(I32)

    def mark(j):
        doc_number = iota((DEVS, LISTS * ELIG), 1)
        hit = slot_ref[:, LANE_CODE + j : LANE_CODE + j + 1] == doc_number
        oh[pl.ds(j * DEVS, DEVS), :] = jnp.where(hit, 1.0, 0.0).astype(BF16)

    def pick(low, high):
        def body(n, carry):
            cols = pl.ds(pl.multiple_of(n * 256, 256), 256)
            block = docs[:, :, cols].reshape(LISTS * ELIG, 256)
            got = jnp.dot(oh[...], block, preferred_element_type=F32)
            gath[:, :, cols] = got.astype(BF16).reshape(CAP, DEVS, 256)
            return carry

        lax.fori_loop(low, high, body, 0)

    def prefix_scores():
        slot_t = slot_ref[...].astype(F32).T
        lists = jnp.concatenate(
            [slot_t[LANE_LIST + p : LANE_LIST + p + 1, :] for p in range(PCAP)], axis=1
        )
        wanted = jnp.concatenate(
            [asked[:, :, pl.ds(p * PREFIX, PREFIX)].reshape(DEVS, PREFIX) for p in range(PCAP)], axis=0
        ).T.astype(BF16)
        sel[...] = jnp.zeros_like(sel)
        for n in range(LISTS):
            got = jnp.dot(dpre[n], wanted, preferred_element_type=F32)
            sel[...] = jnp.where(lists == float(n), got, sel[...])
        rows_valid = jnp.zeros((1, PCAP * DEVS), I32)
        for n in range(LISTS):
            rows_valid = jnp.where(lists == float(n), lengths[n], rows_valid)
        sub = iota((8, DEVS), 0)
        tops = []
        for p in range(PCAP):
            lanes = pl.ds(p * DEVS, DEVS)
            bound = rows_valid[:, p * DEVS : (p + 1) * DEVS]
            seq = [
                jnp.where(sub + v * 8 < bound, sel[pl.ds(v * 8, 8), lanes], LOW) for v in range(32)
            ]
            seq = sort_down(seq)
            for shift in (4, 2, 1):
                seq = join_rolled(seq, shift, 0)
            for m in range(TOPK // 8):
                block = seq[m * 8]
                for s in range(1, 8):
                    block = jnp.where(sub == s, seq[m * 8 + s], block)
                tops.append(block)
        tops.append(jnp.zeros((DEVS - PCAP * TOPK, DEVS), F32))
        psend[...] = jnp.concatenate(tops, axis=0).T.reshape(DEVS, 1, DEVS)

    def return_prefix():
        exchange(psend, precv, 1, True)

    def merge_prefix():
        exchanged(psend, precv, 1)
        precv[own_number] = psend[0]
        back = precv[...].reshape(DEVS, DEVS).T
        first, second = prank == 0.0, prank == 1.0
        seq = [
            jnp.where(
                first, back[k : k + 1, :], jnp.where(second, back[TOPK + k : TOPK + k + 1, :], LOW)
            )
            for k in range(TOPK)
        ]
        for shift in (64, 32, 16, 8, 4, 2, 1):
            seq = join_rolled(seq, shift, 1)
        best = seq[0]
        for k in range(1, TOPK):
            best = jnp.where(lane == k, seq[k], best)
        ptop_ref[...] = best[:, :TOPK]

    def work(stage):
        if stage == 1:
            read_slots()
            for j in range(CAP):
                mark(j)
        elif stage == 2:
            prefix_scores()
            return_prefix()
        elif stage == 3:
            pick(0, 2)
        elif stage == 4:
            pick(2, 4)
        elif stage == 5:
            pick(4, 6)
        elif stage == 6:
            pick(6, 8)
        elif stage == 8:
            merge_prefix()

    gather.run(work)

    group_row = iota((16, 1), 0)
    group_col = iota((16, 256), 1)

    def queries(g, t):
        return qbuf[g // 2, pl.ds(g % 2 * 2, 2), :, :, t].reshape(256, 128)

    def rescore(g, carry):
        here = pl.ds(pl.multiple_of(g * 16, 16), 16)
        rows = slot_ref[here]
        got = jnp.zeros((CAP * 16, 256), F32)
        for k in range(FULL // 256):
            left = gath[:, here, pl.ds(k * 256, 256)].reshape(CAP * 16, 256)
            right = jnp.concatenate([queries(g, 2 * k), queries(g, 2 * k + 1)], axis=1)
            got = got + lax.dot_general(
                left, right, (((1,), (1,)), ((), ())), preferred_element_type=F32
            )
        out = jnp.zeros((16, DEVS), F32)
        for j in range(CAP):
            number = rows[:, LANE_ROW + j : LANE_ROW + j + 1]
            hit = jnp.where(number < 0, -1, group_row * QROWS + number) == group_col
            value = jnp.sum(
                jnp.where(hit, got[j * 16 : (j + 1) * 16, :], 0.0), axis=1, keepdims=True
            )
            out = jnp.where(lane == j, value, out)
        rsend[here] = out.reshape(16, 1, DEVS)
        return carry

    lax.fori_loop(0, 8, rescore, 0, unroll=2)
    exchange(rsend, rrecv, 2, True)
    gather.drain()
    exchanged(rsend, rrecv, 2)
    rrecv[own_number] = rsend[0]
    back = rrecv[...].reshape(DEVS, DEVS).T
    value = jnp.zeros((QROWS, DEVS), F32)
    for j in range(CAP):
        value = jnp.where(srank == float(j), back[j : j + 1, :], value)
    out = jnp.zeros((QROWS, DEVS), F32)
    for s in range(SHORT):
        one = jnp.sum(jnp.where(sdev[:, s : s + 1] == dev, value, 0.0), axis=1, keepdims=True)
        out = jnp.where(lane == s, one, out)
    resc_ref[...] = (out / full_norm)[:, :SHORT]


def shards(queries, probe_dev, probe_list, documents, lengths, short_dev, short_list, short_row):
    vmem = pl.BlockSpec(memory_space=pltpu.VMEM)
    anywhere = pl.BlockSpec(memory_space=pl.ANY)
    return pl.pallas_call(
        kernel,
        name="search",
        out_shape=(
            jax.ShapeDtypeStruct((QROWS, TOPK), F32),
            jax.ShapeDtypeStruct((QROWS, SHORT), F32),
        ),
        in_specs=[anywhere, anywhere, pl.BlockSpec(memory_space=pltpu.SMEM)] + [vmem] * 5,
        out_specs=(vmem, vmem),
        scratch_shapes=[
            pltpu.VMEM((SIDE, SIDE, SIDE, 2, TILES, QROWS, 128), BF16),
            pltpu.VMEM((LISTS, ELIG, FULL), BF16),
            pltpu.VMEM((LISTS, ROWS, PREFIX), BF16),
            pltpu.VMEM((CAP, DEVS, FULL), BF16),
            pltpu.VMEM((CAP * DEVS, LISTS * ELIG), BF16),
            pltpu.VMEM((ROWS, PCAP * DEVS), F32),
            pltpu.VMEM((DEVS, DEVS), I32),
            pltpu.VMEM((DEVS, 1, PCAP * PREFIX + DEVS), F32),
            pltpu.VMEM((DEVS, 1, PCAP * PREFIX + DEVS), F32),
            pltpu.VMEM((DEVS, 1, DEVS), F32),
            pltpu.VMEM((DEVS, 1, DEVS), F32),
            pltpu.VMEM((DEVS, 1, DEVS), F32),
            pltpu.VMEM((DEVS, 1, DEVS), F32),
            pltpu.SemaphoreType.DMA((3,)),
            pltpu.SemaphoreType.DMA,
            pltpu.SemaphoreType.DMA((RINGS * 9,)),
            pltpu.SemaphoreType.DMA,
            pltpu.SemaphoreType.DMA((3,)),
            pltpu.SemaphoreType.DMA((3,)),
        ],
        compiler_params=pltpu.CompilerParams(
            collective_id=0, has_side_effects=True, vmem_limit_bytes=60 * 1024 * 1024
        ),
    )(queries, documents, lengths, short_dev, short_list, short_row, probe_dev, probe_list)


def solution(mesh):
    spread = P(("gx", "gy"), None)
    in_specs = (spread, spread, spread, P(("gx", "gy"), None, None), P(("gx", "gy")), spread, spread, spread)
    return jax.shard_map(shards, mesh=mesh, in_specs=in_specs, out_specs=(spread, spread), check_vma=False)
```

time: 83.9 us -> 57 us (0.68)
  Pallas kernels: 80.4 us -> 53.5 us
    pallas_call x1, Pallas kernels: 80.4 us -> 53.5 us  [shards(): pl.pallas_call(kernel, name='search', out_shape=(jax.ShapeDtypeStruct((QR...]
where the time goes in v2:
time: 57 us; the launch traced here: 56.7 us
  Pallas kernels  53.5 us (94%)
  local copies, waits for them, and re-layouts  2.59 us (5%)
  between operations  0.64 us (1%)
    pallas_call x1, Pallas kernels, shards(): pl.pallas_call(kernel, name='search', out_shape=(jax.ShapeDtypeStruct((QR...  53.5 us
    unnamed x2, local copies, waits for them, and re-layouts  2.59 us

profile of v2, /device:TPU:1, one launch (start us, length us, event | category | flops | bytes accessed | tf_op | source)
XLA Modules:
  0.0 56.7 jit_solution(9664125139384813275)
XLA Ops:
  0.6 53.5 %search.1 = (f32[16,32]{1,0:T(8,128)}, f32[16,32]{1,0:T(8,128)}) custom-call(bf16[16,2048]{1,0:T(8,128)(2,1)} %q_hbm.1, bf16[16,256,2048]{2,1,0:T(8,128)(2,1)} %docs_hbm.1, s32[16]{0:T(128)} %lengths.1, s32[16,32]{1,0:T(8,128)} %sdev_ref.1, s32[16,32]{1,0:T(8,128)} %slist_ref.1, s32[16,32]{1,0:T(8,128)} %srow_ref.1, s32[16,16]{1,0:T(8,128)} %pdev_ref.1, ...), custom_call_target="tpu_custom_call" | custom-call | tf_op jit(solution)/shard_map/search/pallas_call | solution.py:497
  54.1 1.3 %copy.12 = f32[16,32]{1,0:T(8,128)} copy(f32[16,32]{1,0:T(8,128)} %get-tuple-element.4) | data formatting | bytes 4096
  55.4 1.3 %copy.13 = f32[16,32]{1,0:T(8,128)} copy(f32[16,32]{1,0:T(8,128)} %get-tuple-element.5) | data formatting | bytes 4096

commit v3 on v2

v3 whole, which is shorter than its diff:
```python
import jax
import jax.numpy as jnp
from jax import lax
from jax.experimental import pallas as pl
from jax.experimental.pallas import tpu as pltpu
from jax.sharding import PartitionSpec as P

MESH = pl.DeviceIdType.MESH
SIDE = 4
DEVS = 128
QROWS = 16
LISTS = 16
ROWS = 256
ELIG = 96
PREFIX = 256
FULL = 2048
TILES = FULL // 128
CAP = 5
PCAP = 2
TOPK = 32
SHORT = 32
PROBES = 16
LOW = -1e30
PARTS = ((0, 2, 2), (2, 7, 0), (7, 12, 1), (12, 16, 2))
F32 = jnp.float32
BF16 = jnp.bfloat16
I32 = jnp.int32
LANE_CODE, LANE_ROW, LANE_LIST, LANE_PROW = 0, 5, 10, 12
RINGS = 8


def iota(shape, axis):
    return lax.broadcasted_iota(I32, shape, axis)


def merge_down(seq):
    seq = list(seq)
    step = len(seq) // 2
    while step:
        for i in range(len(seq)):
            if not i & step:
                a, b = seq[i], seq[i + step]
                seq[i], seq[i + step] = jnp.maximum(a, b), jnp.minimum(a, b)
        step //= 2
    return seq


def sort_down(seq):
    if len(seq) == 1:
        return list(seq)
    half = len(seq) // 2
    return merge_down(sort_down(seq[:half]) + sort_down(seq[half:])[::-1])


def join_rolled(seq, shift, axis):
    count = len(seq)
    other = [pltpu.roll(v, shift, axis) for v in seq]
    return merge_down([jnp.maximum(seq[i], other[count - 1 - i]) for i in range(count)])


def coords():
    gx, gy = lax.axis_index("gx"), lax.axis_index("gy")
    return gx // SIDE, gx % SIDE, gy // 2, gy % 2


def device_of(y, x, z, c):
    return (y * SIDE + x, z * 2 + c)


FAR_FIRST = (2, 1, 3, 0)
EVERY, REST = slice(0, SIDE), slice(1, SIDE)
NEAR, FAR = (("C2", 3), ("C3", 1)), (("C4", 2),)


class Peers:
    def __init__(self, me):
        self.rows = [(me[0] + d) % SIDE * SIDE for d in range(SIDE)]
        self.xs = [(me[1] + d) % SIDE for d in range(SIDE)]
        zs = [(me[2] + d) % SIDE * 2 for d in range(SIDE)]
        self.gys = [[z + me[3], z + 1 - me[3]] for z in zs]
        self.me = me

    def each(self, visit):
        def visit_one(dy, back_dy, gx, dx, dz, dc):
            gy = self.gys[dz][dc]
            off = dy * 16 + (dc * 64 + dx * 4 + dz)
            back = back_dy * 16 + (dc * 64 + (SIDE - dx) % SIDE * 4 + (SIDE - dz) % SIDE)
            visit((gx, gy), gx * 8 + gy, off, back)

        def plane(number, carry):
            dy = (number + 2) % SIDE
            row = (self.me[0] + dy) % SIDE * SIDE
            for dx in FAR_FIRST:
                gx = row + self.xs[dx]
                for dz in FAR_FIRST:
                    for dc in range(2):
                        if dx or dz or dc:
                            visit_one(dy, (SIDE - dy) % SIDE, gx, dx, dz, dc)
            return carry

        lax.fori_loop(0, SIDE, plane, 0)
        for dy in range(1, SIDE):
            visit_one(dy, SIDE - dy, self.rows[dy] + self.xs[0], 0, 0, 0)

    def group(self, g):
        for dx in FAR_FIRST:
            for dz in FAR_FIRST:
                if g or dx or dz:
                    yield dx // 2, (self.rows[g % SIDE] + self.xs[dx], self.gys[dz][g // SIDE])


class Gather:
    def __init__(self, qbuf, send_sem, recv_sem, cross_sem, me):
        self.qbuf, self.send_sem, self.recv_sem = qbuf, send_sem, recv_sem
        self.cross_sem, self.me = cross_sem, me
        self.count = 0
        y, x, z, c = me
        self.partner = device_of(y, x, z, 1 - c)
        self.peers = {}
        for axis in range(3):
            for step in (1, 2, 3):
                place = list(me)
                place[axis] = (place[axis] + step) % SIDE
                self.peers[axis, step] = device_of(*place)

    def view(self, where, tiles, core=0):
        return self.qbuf.at[where[0], where[1], where[2], core, tiles]

    def next_sem(self):
        self.count += 1
        return self.recv_sem.at[self.count - 1]

    def start(self, src, dst, peer, sem):
        copy = pltpu.make_async_remote_copy(
            src_ref=src, dst_ref=dst, send_sem=self.send_sem, recv_sem=sem,
            device_id=peer, device_id_type=MESH,
        )
        copy.start()
        return copy

    def slot(self, ring, value, tiles):
        where = list(ring["unit"])
        where[ring["axis"]] = value
        return self.view(where, tiles)

    def ring_start(self, unit, axis, tiles, far=False):
        ring = dict(unit=unit, axis=axis, tiles=tiles, end=self.next_sem())
        own = self.slot(ring, 0, tiles)
        ring["fwd"] = self.start(own, self.slot(ring, 3, tiles), self.peers[axis, 1], self.next_sem())
        ring["bwd"] = self.start(own, self.slot(ring, 1, tiles), self.peers[axis, 3], self.next_sem())
        if far:
            self.start(own, self.slot(ring, 2, tiles), self.peers[axis, 2], ring["end"])
        return ring

    def ring_low(self, ring, relay=True):
        ring["fwd"].wait_recv()
        if relay:
            tiles = slice(ring["tiles"].start, (ring["tiles"].start + ring["tiles"].stop) // 2)
            src, dst = self.slot(ring, 3, tiles), self.slot(ring, 2, tiles)
            self.start(src, dst, self.peers[ring["axis"], 1], ring["end"])

    def ring_high(self, ring, relay=True):
        ring["bwd"].wait_recv()
        if relay:
            tiles = slice((ring["tiles"].start + ring["tiles"].stop) // 2, ring["tiles"].stop)
            src, dst = self.slot(ring, 1, tiles), self.slot(ring, 2, tiles)
            self.start(src, dst, self.peers[ring["axis"], 3], ring["end"])

    def ring_end(self, ring):
        far = self.slot(ring, 2, ring["tiles"])
        pltpu.make_async_copy(far, far, ring["end"]).wait()

    def across(self, part, where):
        tiles = part["tiles"]
        self.start(
            self.view(where, tiles, 0), self.view(where, tiles, 1), self.partner, self.cross_sem.at[part["late"]]
        )

    def unit(self, part, a, b, c):
        where = [0, 0, 0]
        for axis, value in zip(part["axes"], (a, b, c)):
            where[axis] = value
        return where

    def to_c(self, part, name, a, b):
        where = self.unit(part, a, b, 0)
        part[name] = self.ring_start(where, part["axes"][2], part["tiles"])
        self.across(part, where)

    def begin(self):
        self.parts = []
        for low, high, first in PARTS:
            axes = (first, (first + 1) % 3, (first + 2) % 3)
            self.parts.append(dict(axes=axes, tiles=slice(low, high), late=int(low > 0)))
        home = [0, 0, 0]
        for part in self.parts:
            part["A"] = self.ring_start(home, part["axes"][0], part["tiles"], far=True)
        for name, order in (("B0", 1), ("C0", 2)):
            for part in self.parts:
                part[name] = self.ring_start(home, part["axes"][order], part["tiles"])
        for part in self.parts:
            self.across(part, home)

    def first_axis(self, parts):
        for part in parts:
            self.ring_low(part["A"], relay=False)
            self.ring_high(part["A"], relay=False)
            self.ring_end(part["A"])
            part["B1"] = self.ring_start(self.unit(part, REST, 0, 0), part["axes"][1], part["tiles"])

    def home_blocks(self, parts):
        for name in ("B0", "C0"):
            for part in parts:
                self.ring_low(part[name])
                self.ring_high(part[name])
        for part in parts:
            self.to_c(part, "C1", REST, 0)

    def second_axis(self, parts):
        for part in parts:
            self.ring_low(part["B1"])
            self.ring_high(part["B1"])
        for part in parts:
            self.to_c(part, "C2", EVERY, 3)
            self.to_c(part, "C3", EVERY, 1)

    def second_axis_end(self, parts):
        for part in parts:
            self.ring_end(part["B0"])
            self.ring_end(part["B1"])
            self.to_c(part, "C4", EVERY, 2)

    def third_axis_line(self, parts):
        for part in parts:
            self.ring_low(part["C1"])
            self.ring_high(part["C1"])

    def third_axis(self, parts, pairs):
        for name, b in pairs:
            for part in parts:
                self.ring_low(part[name])
                self.ring_high(part[name])
                self.across(part, self.unit(part, EVERY, b, 3))
                self.across(part, self.unit(part, EVERY, b, 1))

    def third_axis_line_end(self, parts):
        for part in parts:
            self.ring_end(part["C0"])
            self.across(part, self.unit(part, 0, 0, REST))
            self.ring_end(part["C1"])
            self.across(part, self.unit(part, REST, 0, REST))

    def third_axis_end(self, parts, pairs):
        for name, b in pairs:
            for part in parts:
                self.ring_end(part[name])
                self.across(part, self.unit(part, EVERY, b, 2))

    def wait_partner(self, late):
        low = PARTS[0][1]
        tiles = slice(low, TILES) if late else slice(0, low)
        half = self.qbuf.at[:, :, :, 1, tiles]
        pltpu.make_async_copy(half, half, self.cross_sem.at[late]).wait()

    def drain(self):
        rest = slice(1, SIDE)
        for ref in (
            self.qbuf.at[rest], self.qbuf.at[0, rest], self.qbuf.at[0, 0, rest], self.qbuf.at[0, 0, 0, 1]
        ):
            pltpu.make_async_copy(ref, ref, self.send_sem).wait()


def kernel(
    q_hbm, docs_hbm, lengths_hbm, sdev_hbm, slist_hbm, srow_hbm, pdev_hbm, plist_hbm,
    out_ref,
    lengths, sdev_ref, slist_ref, srow_ref, pdev_ref, plist_ref,
    qbuf, docs, dpre, gath, oh, sel, slot_ref, psel, ask, asked, psend, precv, rsend, rrecv,
    small_sem, load_sem, gsend, grecv, gcross, xsend, xrecv,
):
    me = coords()
    own_number = (me[0] * SIDE + me[1]) * 8 + me[2] * 2 + me[3]
    peers = Peers(me)
    barrier = pltpu.get_barrier_semaphore()
    small = [
        pltpu.make_async_copy(src, dst, small_sem.at[n])
        for n, (src, dst) in enumerate((
            (sdev_hbm, sdev_ref), (slist_hbm, slist_ref), (srow_hbm, srow_ref),
            (pdev_hbm, pdev_ref), (plist_hbm, plist_ref), (lengths_hbm, lengths),
        ))
    ]
    for copy in small:
        copy.start()
    for t in range(TILES):
        pltpu.make_async_copy(
            q_hbm.at[:, pl.ds(t * 128, 128)], qbuf.at[0, 0, 0, 0, t], load_sem.at[0]
        ).start()

    def greet(peer, flat, off, back):
        pl.semaphore_signal(barrier, inc=1, device_id=peer, device_id_type=MESH)

    peers.each(greet)
    docs_copy = pltpu.make_async_copy(docs_hbm.at[:, pl.ds(0, ELIG), :], docs, load_sem.at[1])
    docs_copy.start()
    dpre_copy = pltpu.make_async_copy(docs_hbm.at[:, :, pl.ds(0, PREFIX)], dpre, load_sem.at[2])
    dpre_copy.start()
    for copy in small:
        copy.wait()

    dev = iota((QROWS, DEVS), 1)
    sdev = sdev_ref[...]
    scode = (slist_ref[...] * ELIG + srow_ref[...] + 1).astype(F32)
    pdev = pdev_ref[...]
    pcode = (plist_ref[...] + 1).astype(F32)
    lower = (iota((QROWS, QROWS), 1) < iota((QROWS, QROWS), 0)).astype(F32).astype(BF16)
    qnum = iota((QROWS, DEVS), 0).astype(F32) + 1.0

    def table(devs, codes, width):
        got = jnp.zeros((QROWS, DEVS), F32)
        for s in range(width):
            got = got + jnp.where(devs[:, s : s + 1] == dev, codes[:, s : s + 1], 0.0)
        used = jnp.where(got > 0.0, 1.0, 0.0)
        rank = jnp.dot(lower, used.astype(BF16), preferred_element_type=F32)
        return got, jnp.where(used > 0.0, rank, -1.0)

    stab, srank = table(sdev, scode, SHORT)
    ptab, prank = table(pdev, pcode, PROBES)
    krow = iota((16, DEVS), 0)
    slots = jnp.zeros((16, DEVS), F32)
    for base, row_base, tab, rank, cap in (
        (LANE_CODE, LANE_ROW, stab, srank, CAP),
        (LANE_LIST, LANE_PROW, ptab, prank, PCAP),
    ):
        for j in range(cap):
            hit = rank == float(j)
            code = jnp.sum(jnp.where(hit, tab, 0.0), axis=0, keepdims=True) - 1.0
            row = jnp.sum(jnp.where(hit, qnum, 0.0), axis=0, keepdims=True) - 1.0
            slots = jnp.where(krow == base + j, code, slots)
            slots = jnp.where(krow == row_base + j, row, slots)
    slots = jnp.concatenate([slots, jnp.zeros((112, DEVS), F32)], axis=0).T
    ask[...] = slots.astype(I32).reshape(DEVS, 1, DEVS)

    pltpu.make_async_copy(qbuf.at[0, 0, 0, 1], qbuf.at[0, 0, 0, 0], load_sem.at[0]).wait()
    pl.semaphore_wait(barrier, DEVS - 1)
    gather = Gather(qbuf, gsend, grecv, gcross, me)
    gather.begin()
    def exchange(send, recv, number, by_offset):
        def visit(peer, flat, off, back):
            if by_offset:
                src, dst = send.at[off], recv.at[own_number]
            else:
                src, dst = send.at[flat], recv.at[back]
            pltpu.make_async_remote_copy(
                src_ref=src, dst_ref=dst, send_sem=xsend.at[number], recv_sem=xrecv.at[number],
                device_id=peer, device_id_type=MESH,
            ).start()

        peers.each(visit)

    def exchanged(send, recv, number):
        rest = pl.ds(0, DEVS - 1)
        pltpu.make_async_copy(recv.at[rest], recv.at[rest], xrecv.at[number]).wait()
        pltpu.make_async_copy(send.at[rest], send.at[rest], xsend.at[number]).wait()

    exchange(ask, asked, 0, False)

    lane = iota((16, DEVS), 1)

    def read_slots():
        exchanged(ask, asked, 0)
        asked[0] = ask[own_number]
        docs_copy.wait()
        dpre_copy.wait()
        slot_ref[...] = asked[...].reshape(DEVS, DEVS)

    def mark(j):
        doc_number = iota((DEVS, LISTS * ELIG), 1)
        hit = slot_ref[:, LANE_CODE + j : LANE_CODE + j + 1] == doc_number
        oh[pl.ds(j * DEVS, DEVS), :] = jnp.where(hit, 1.0, 0.0).astype(BF16)

    def pick(low, high):
        def body(n, carry):
            cols = pl.ds(pl.multiple_of(n * 256, 256), 256)
            block = docs[:, :, cols].reshape(LISTS * ELIG, 256)
            got = jnp.dot(oh[...], block, preferred_element_type=F32)
            gath[:, :, cols] = got.astype(BF16).reshape(CAP, DEVS, 256)
            return carry

        lax.fori_loop(low, high, body, 0)

    group_row = iota((16, 1), 0)
    group_col = iota((16, 256), 1)

    def queries(g, low, high):
        tiles = [qbuf[g % SIDE, :, :, g // SIDE, t].reshape(256, 128) for t in range(low, high)]
        return jnp.concatenate(tiles, axis=1)

    def column(g, at):
        number = slot_ref[pl.ds(g * 16, 16), at : at + 1]
        return jnp.where(number < 0, -1, group_row * QROWS + number)

    def prefix_scores():
        for g in range(2 * SIDE):
            hits = [jnp.where(column(g, LANE_PROW + p) == group_col, 1.0, 0.0) for p in range(PCAP)]
            hit = jnp.concatenate(hits, axis=0).astype(BF16)
            rows = jnp.dot(hit, queries(g, 0, PREFIX // 128), preferred_element_type=F32)
            norm = jnp.sqrt(1.0 + jnp.sum(rows * rows, axis=1, keepdims=True))
            rows = rows / norm
            for p in range(PCAP):
                psel[pl.ds(p * DEVS + g * 16, 16), :] = rows[p * 16 : (p + 1) * 16, :]
        slot_t = slot_ref[...].astype(F32).T
        lists = jnp.concatenate(
            [slot_t[LANE_LIST + p : LANE_LIST + p + 1, :] for p in range(PCAP)], axis=1
        )
        wanted = psel[...].T.astype(BF16)
        sel[...] = jnp.zeros_like(sel)
        for n in range(LISTS):
            got = jnp.dot(dpre[n], wanted, preferred_element_type=F32)
            sel[...] = jnp.where(lists == float(n), got, sel[...])
        rows_valid = jnp.zeros((1, PCAP * DEVS), I32)
        for n in range(LISTS):
            rows_valid = jnp.where(lists == float(n), lengths[n], rows_valid)
        sub = iota((8, DEVS), 0)
        tops = []
        for p in range(PCAP):
            lanes = pl.ds(p * DEVS, DEVS)
            bound = rows_valid[:, p * DEVS : (p + 1) * DEVS]
            seq = [
                jnp.where(sub + v * 8 < bound, sel[pl.ds(v * 8, 8), lanes], LOW) for v in range(32)
            ]
            seq = sort_down(seq)
            for shift in (4, 2, 1):
                seq = join_rolled(seq, shift, 0)
            for m in range(TOPK // 8):
                block = seq[m * 8]
                for s in range(1, 8):
                    block = jnp.where(sub == s, seq[m * 8 + s], block)
                tops.append(block)
        tops.append(jnp.zeros((DEVS - PCAP * TOPK, DEVS), F32))
        psend[...] = jnp.concatenate(tops, axis=0).T.reshape(DEVS, 1, DEVS)

    def return_prefix():
        exchange(psend, precv, 1, True)

    def merge_prefix():
        exchanged(psend, precv, 1)
        precv[own_number] = psend[0]
        back = precv[...].reshape(DEVS, DEVS).T
        first, second = prank == 0.0, prank == 1.0
        seq = [
            jnp.where(
                first, back[k : k + 1, :], jnp.where(second, back[TOPK + k : TOPK + k + 1, :], LOW)
            )
            for k in range(TOPK)
        ]
        for shift in (64, 32, 16, 8, 4, 2, 1):
            seq = join_rolled(seq, shift, 1)
        best = seq[0]
        for k in range(1, TOPK):
            best = jnp.where(lane == k, seq[k], best)
        out_ref[...] = best

    first, others = gather.parts[:1], gather.parts[1:]
    gather.first_axis(first)
    gather.first_axis(others)
    gather.home_blocks(first)
    gather.home_blocks(others)
    gather.second_axis(first)
    read_slots()
    for j in range(CAP):
        mark(j)
    gather.second_axis(others)
    gather.third_axis_line(first)
    gather.second_axis_end(first)
    pick(0, 2)
    gather.third_axis_line(others)
    gather.third_axis(first, NEAR)
    gather.second_axis_end(others)
    gather.third_axis(first, FAR)
    gather.third_axis_line_end(first)
    pick(2, 4)
    gather.third_axis(others, NEAR)
    gather.third_axis_end(first, NEAR)
    gather.third_axis_end(first, FAR)
    pick(4, 6)
    gather.third_axis(others, FAR)
    gather.wait_partner(0)
    prefix_scores()
    return_prefix()
    gather.third_axis_line_end(others)
    gather.third_axis_end(others, NEAR)
    pick(6, 8)
    gather.third_axis_end(others, FAR)

    def rescore(groups):
        for g in groups:
            left = gath[:, pl.ds(g * 16, 16), :].reshape(CAP * 16, FULL)
            got = lax.dot_general(
                left, queries(g, 0, TILES), (((1,), (1,)), ((), ())), preferred_element_type=F32
            )
            total = jnp.zeros((16, 256), F32)
            for j in range(CAP):
                hit = column(g, LANE_ROW + j) == group_col
                total = total + jnp.where(hit, got[j * 16 : (j + 1) * 16, :], 0.0)
            value = jnp.sum(total, axis=0, keepdims=True)
            for half in range(2):
                rsend[g * 2 + half] = value[:, half * 128 : (half + 1) * 128]
        for g in groups:
            for half, peer in peers.group(g):
                pltpu.make_async_remote_copy(
                    src_ref=rsend.at[g * 2 + half], dst_ref=rrecv.at[own_number],
                    send_sem=xsend.at[2], recv_sem=xrecv.at[2], device_id=peer, device_id_type=MESH,
                ).start()

    rescore((2, 1))
    rescore((3, 0))
    gather.wait_partner(1)
    rescore((6, 5))
    rescore((7, 4))
    gather.drain()
    merge_prefix()
    exchanged(rrecv, rrecv, 2)
    squares = jnp.zeros((QROWS, 128), F32)
    for t in range(TILES):
        value = qbuf[0, 0, 0, 0, t].astype(F32)
        squares = squares + value * value
    full_norm = jnp.sqrt(1.0 + jnp.sum(squares, axis=1, keepdims=True))
    rrecv[own_number] = rsend[0]
    back = rrecv[...].reshape(DEVS, DEVS).T
    other = iota((16, DEVS), 1)
    other_x, other_z = other // 8 % SIDE, other // 2 % SIDE
    place = (me[1] + SIDE - other_x) % 2 * SIDE + (me[2] + SIDE - other_z) % SIDE
    value = jnp.zeros((QROWS, DEVS), F32)
    for n in range(8):
        value = jnp.where(place == n, back[n * 16 : (n + 1) * 16, :], value)
    out = jnp.zeros((QROWS, DEVS), F32)
    for s in range(SHORT):
        one = jnp.sum(jnp.where(sdev[:, s : s + 1] == dev, value, 0.0), axis=1, keepdims=True)
        out = jnp.where(lane == s, one, out)
    out_ref[:, pl.ds(TOPK, SHORT)] = (out / full_norm)[:, :SHORT]


def shards(queries, probe_dev, probe_list, documents, lengths, short_dev, short_list, short_row):
    vmem = pl.BlockSpec(memory_space=pltpu.VMEM)
    anywhere = pl.BlockSpec(memory_space=pl.ANY)
    out = pl.pallas_call(
        kernel,
        name="search",
        out_shape=pltpu.VMEM((QROWS, DEVS), F32),
        in_specs=[anywhere] * 8,
        out_specs=vmem,
        scratch_shapes=[
            pltpu.SMEM((LISTS,), I32),
            pltpu.VMEM((QROWS, SHORT), I32),
            pltpu.VMEM((QROWS, SHORT), I32),
            pltpu.VMEM((QROWS, SHORT), I32),
            pltpu.VMEM((QROWS, PROBES), I32),
            pltpu.VMEM((QROWS, PROBES), I32),
            pltpu.VMEM((SIDE, SIDE, SIDE, 2, TILES, QROWS, 128), BF16),
            pltpu.VMEM((LISTS, ELIG, FULL), BF16),
            pltpu.VMEM((LISTS, ROWS, PREFIX), BF16),
            pltpu.VMEM((CAP, DEVS, FULL), BF16),
            pltpu.VMEM((CAP * DEVS, LISTS * ELIG), BF16),
            pltpu.VMEM((ROWS, PCAP * DEVS), F32),
            pltpu.VMEM((DEVS, DEVS), I32),
            pltpu.VMEM((PCAP * DEVS, PREFIX), F32),
            pltpu.VMEM((DEVS, 1, DEVS), I32),
            pltpu.VMEM((DEVS, 1, DEVS), I32),
            pltpu.VMEM((DEVS, 1, DEVS), F32),
            pltpu.VMEM((DEVS, 1, DEVS), F32),
            pltpu.VMEM((4 * SIDE, 1, DEVS), F32),
            pltpu.VMEM((DEVS, 1, DEVS), F32),
            pltpu.SemaphoreType.DMA((6,)),
            pltpu.SemaphoreType.DMA((3,)),
            pltpu.SemaphoreType.DMA,
            pltpu.SemaphoreType.DMA((RINGS * 3 * len(PARTS),)),
            pltpu.SemaphoreType.DMA((2,)),
            pltpu.SemaphoreType.DMA((3,)),
            pltpu.SemaphoreType.DMA((3,)),
        ],
        compiler_params=pltpu.CompilerParams(
            collective_id=0, has_side_effects=True, vmem_limit_bytes=60 * 1024 * 1024
        ),
    )(queries, documents, lengths, short_dev, short_list, short_row, probe_dev, probe_list)
    return out[:, :TOPK], out[:, TOPK : TOPK + SHORT]


def solution(mesh):
    spread = P(("gx", "gy"), None)
    in_specs = (spread, spread, spread, P(("gx", "gy"), None, None), P(("gx", "gy")), spread, spread, spread)
    return jax.shard_map(shards, mesh=mesh, in_specs=in_specs, out_specs=(spread, spread), check_vma=False)
```

time: 57 us -> 46.6 us (0.82)
  Pallas kernels: 53.5 us -> 45.1 us
  local copies, waits for them, and re-layouts: 2.59 us -> 0.67 us
    pallas_call x1, Pallas kernels: 53.5 us -> 45.1 us  [shards(): pl.pallas_call(kernel, name='search', out_shape=pltpu.VMEM((QROWS, DEVS),...]
    unnamed x2 -> x0, local copies, waits for them, and re-layouts: 2.59 us -> none
    slice x0 -> x1, local copies, waits for them, and re-layouts: none -> 0.67 us  [shards(): return (out[:, :TOPK], out[:, TOPK:TOPK + SHORT])]
where the time goes in v3:
time: 46.6 us; the launch traced here: 46.5 us
  Pallas kernels  45.1 us (97%)
  local copies, waits for them, and re-layouts  0.67 us (1%)
  between operations  0.64 us (1%)
    pallas_call x1, Pallas kernels, shards(): pl.pallas_call(kernel, name='search', out_shape=pltpu.VMEM((QROWS, DEVS),...  45.1 us

profile of v3, /device:TPU:1, one launch (start us, length us, event | category | flops | bytes accessed | tf_op | source)
XLA Modules:
  0.0 46.5 jit_solution(18142651460093086704)
XLA Ops:
  0.6 45.1 %search.1 = f32[16,128]{1,0:T(8,128)S(1)} custom-call(bf16[16,2048]{1,0:T(8,128)(2,1)} %q_hbm.1, bf16[16,256,2048]{2,1,0:T(8,128)(2,1)} %docs_hbm.1, s32[16]{0:T(128)} %lengths_hbm.1, s32[16,32]{1,0:T(8,128)} %sdev_hbm.1, s32[16,32]{1,0:T(8,128)} %slist_hbm.1, s32[16,32]{1,0:T(8,128)} %srow_hbm.1, s32[16,16]{1,0:T(8,128)} %pdev_hbm.1, s32[16,16]{1,0:T(8,128)} %plist_hbm.1), custom_call_target="tpu_custom_call" | custom-call | tf_op jit(solution)/shard_map/search/pallas_call | solution.py:545
  45.8 0.7 %fusion = (f32[16,32]{1,0:T(8,128)}, f32[16,32]{1,0:T(8,128)}) fusion(f32[16,128]{1,0:T(8,128)S(1)} %search.1), kind=kLoop, calls=%fused_computation | loop fusion | bytes 8192 | tf_op jit(solution)/shard_map/slice | solution.py:584

commit v4 on v3

v4 whole, which is shorter than its diff:
```python
import jax
import jax.numpy as jnp
from jax import lax
from jax.experimental import pallas as pl
from jax.experimental.pallas import tpu as pltpu
from jax.sharding import PartitionSpec as P

MESH = pl.DeviceIdType.MESH
SIDE = 4
DEVS = 128
QROWS = 16
LISTS = 16
ROWS = 256
ELIG = 96
PREFIX = 256
FULL = 2048
TILES = FULL // 128
CAP = 5
PCAP = 2
TOPK = 32
SHORT = 32
PROBES = 16
LOW = -1e30
PARTS = ((0, 2, 2), (2, 7, 0), (7, 12, 1), (12, 16, 2))
F32 = jnp.float32
BF16 = jnp.bfloat16
I32 = jnp.int32
LANE_CODE, LANE_ROW, LANE_LIST, LANE_PROW = 0, 5, 10, 12


def iota(shape, axis):
    return lax.broadcasted_iota(I32, shape, axis)


def merge_down(seq):
    seq = list(seq)
    step = len(seq) // 2
    while step:
        for i in range(len(seq)):
            if not i & step:
                a, b = seq[i], seq[i + step]
                seq[i], seq[i + step] = jnp.maximum(a, b), jnp.minimum(a, b)
        step //= 2
    return seq


def sort_down(seq):
    if len(seq) == 1:
        return list(seq)
    half = len(seq) // 2
    return merge_down(sort_down(seq[:half]) + sort_down(seq[half:])[::-1])


def join_rolled(seq, shift, axis):
    count = len(seq)
    other = [pltpu.roll(v, shift, axis) for v in seq]
    return merge_down([jnp.maximum(seq[i], other[count - 1 - i]) for i in range(count)])


def coords():
    gx, gy = lax.axis_index("gx"), lax.axis_index("gy")
    return gx // SIDE, gx % SIDE, gy // 2, gy % 2


def device_of(y, x, z, c):
    return (y * SIDE + x, z * 2 + c)


FAR_FIRST = (2, 1, 3, 0)
BLOCKS = sorted(
    ((y, x, z) for y in range(SIDE) for x in range(SIDE) for z in range(SIDE)),
    key=lambda b: (min(2, sum(v == 2 for v in b)), b),
)
CHIPS = len(BLOCKS)
HALF = CHIPS // 2
WAVES = ((0, 27), (27, 54), (54, 64))
WAVE_ROWS = (4, 4, 2)
EVERY, REST = slice(0, SIDE), slice(1, SIDE)
NEAR, FAR = (("C2", 3), ("C3", 1)), (("C4", 2),)
NEAR_SEM = dict(A="A", B0="B0", C0="C0", B1="B1", C1="C1", C2="C23", C3="C23", C4="C4")
END_SEM = dict(A="A", B0="B_", B1="B_", C0="C01_", C1="C01_", C2="C23_", C3="C23_", C4="C4_")
STRAIGHT_FIRST, STRAIGHT = ("A", "B0", "B1", "C4"), ("A",)


class Peers:
    def __init__(self, me):
        rows = [(me[0] + d) % SIDE * SIDE for d in range(SIDE)]
        xs = [(me[1] + d) % SIDE for d in range(SIDE)]
        zs = [(me[2] + d) % SIDE * 2 for d in range(SIDE)]
        self.gxs = [[row + x for x in xs] for row in rows]
        self.gys = [[z + me[3], z + 1 - me[3]] for z in zs]

    def at(self, off):
        y, x, z = BLOCKS[off % CHIPS]
        return self.gxs[y][x], self.gys[z][off // CHIPS]

    def each(self, visit, near_half_first=False):
        def order(off):
            return near_half_first and off % CHIPS // HALF, -sum(min(v, SIDE - v) for v in BLOCKS[off % CHIPS])

        for off in sorted(range(1, DEVS), key=order):
            gx, gy = self.at(off)
            back = tuple((SIDE - v) % SIDE for v in BLOCKS[off % CHIPS])
            visit((gx, gy), gx * 8 + gy, off, off // CHIPS * CHIPS + BLOCKS.index(back))


class Gather:
    def __init__(self, qbuf, send_sem, recv_sem, cross_sem, me):
        self.qbuf, self.send_sem, self.recv_sem = qbuf, send_sem, recv_sem
        self.cross_sem, self.me = cross_sem, me
        self.sems = {}
        y, x, z, c = me
        self.partner = device_of(y, x, z, 1 - c)
        self.peers = {}
        for axis in range(3):
            for step in (1, 2, 3):
                place = list(me)
                place[axis] = (place[axis] + step) % SIDE
                self.peers[axis, step] = device_of(*place)

    def view(self, where, tiles, core=0):
        return self.qbuf.at[where[0], where[1], where[2], core, tiles]

    def start(self, src, dst, peer, sem):
        pltpu.make_async_remote_copy(
            src_ref=src, dst_ref=dst, send_sem=self.send_sem, recv_sem=sem,
            device_id=peer, device_id_type=MESH,
        ).start()

    def sem(self, part, name):
        key = part["number"], name
        if key not in self.sems:
            self.sems[key] = len(self.sems)
        return self.recv_sem.at[self.sems[key]]

    def slot(self, part, name, value, tiles=None):
        unit, axis = part[name]
        where = list(unit)
        where[axis] = value
        return self.view(where, tiles or part["tiles"])

    def ring_start(self, part, name, order, a, b):
        axis = part["axes"][order]
        part[name] = self.unit(part, a, b, 0), axis
        own = self.slot(part, name, 0)
        near = self.sem(part, NEAR_SEM[name])
        self.start(own, self.slot(part, name, 3), self.peers[axis, 1], near)
        self.start(own, self.slot(part, name, 1), self.peers[axis, 3], near)
        if self.straight(part, name):
            self.start(own, self.slot(part, name, 2), self.peers[axis, 2], self.sem(part, END_SEM[name]))

    def straight(self, part, name):
        return name in (STRAIGHT_FIRST if part["number"] == 0 else STRAIGHT)

    def wait(self, ref, sem):
        pltpu.make_async_copy(ref, ref, sem).wait()

    def near(self, part, names):
        self.wait(self.as_many(part, names, slice(1, 3)), self.sem(part, NEAR_SEM[names[0]]))
        tiles = part["tiles"]
        middle = (tiles.start + tiles.stop) // 2
        for name in names:
            if self.straight(part, name):
                continue
            end = self.sem(part, END_SEM[name])
            axis = part[name][1]
            for value, step, piece in ((3, 1, slice(tiles.start, middle)), (1, 3, slice(middle, tiles.stop))):
                self.start(
                    self.slot(part, name, value, piece), self.slot(part, name, 2, piece), self.peers[axis, step], end
                )

    def end(self, part, names):
        self.wait(self.as_many(part, names, 2), self.sem(part, END_SEM[names[0]]))

    def as_many(self, part, names, value):
        unit, axis = part[names[0]]
        where = list(unit)
        where[axis] = value
        if names in (("B0", "B1"), ("C0", "C1")):
            where[part["axes"][0]] = EVERY
        elif len(names) > 1:
            where[part["axes"][1]] = slice(0, len(names))
        return self.view(where, part["tiles"])

    def across(self, part, where, wave):
        tiles = part["tiles"]
        sem = self.cross_sem.at[wave + 1 if part["number"] or wave == 0 else 0]
        self.start(self.view(where, tiles, 0), self.view(where, tiles, 1), self.partner, sem)

    def unit(self, part, a, b, c):
        where = [0, 0, 0]
        for axis, value in zip(part["axes"], (a, b, c)):
            where[axis] = value
        return where

    def to_c(self, part, name, a, b):
        self.ring_start(part, name, 2, a, b)
        self.across(part, self.unit(part, a, b, 0), int(b == 2))

    def begin(self):
        self.parts = []
        for number, (low, high, first) in enumerate(PARTS):
            axes = (first, (first + 1) % 3, (first + 2) % 3)
            self.parts.append(dict(number=number, axes=axes, tiles=slice(low, high)))
        for order, name in enumerate(("A", "B0", "C0")):
            for part in self.parts:
                self.ring_start(part, name, order, 0, 0)
        for part in self.parts:
            self.across(part, [0, 0, 0], 0)

    def first_axis(self, parts):
        for part in parts:
            self.wait(self.as_many(part, ("A",), REST), self.sem(part, "A"))
            self.ring_start(part, "B1", 1, REST, 0)

    def home_blocks(self, parts):
        for name in ("B0", "C0"):
            for part in parts:
                self.near(part, (name,))
        for part in parts:
            self.to_c(part, "C1", REST, 0)

    def second_axis(self, parts):
        for part in parts:
            self.near(part, ("B1",))
        for part in parts:
            self.to_c(part, "C2", EVERY, 3)
            self.to_c(part, "C3", EVERY, 1)

    def second_axis_end(self, parts):
        for part in parts:
            self.end(part, ("B0", "B1"))
            self.to_c(part, "C4", EVERY, 2)

    def third_axis_line(self, parts):
        for part in parts:
            self.near(part, ("C1",))
            self.across(part, self.unit(part, EVERY, 0, 3), 0)
            self.across(part, self.unit(part, EVERY, 0, 1), 0)

    def third_axis(self, parts, pairs):
        for part in parts:
            self.near(part, tuple(name for name, _ in pairs))
            for _, b in pairs:
                self.across(part, self.unit(part, EVERY, b, 3), int(b == 2))
                self.across(part, self.unit(part, EVERY, b, 1), int(b == 2))

    def third_axis_line_end(self, parts):
        for part in parts:
            self.end(part, ("C0", "C1"))
            self.across(part, self.unit(part, EVERY, 0, 2), 1)

    def third_axis_end(self, parts, pairs):
        for part in parts:
            self.end(part, tuple(name for name, _ in pairs))
            for _, b in pairs:
                self.across(part, self.unit(part, EVERY, b, 2), 1 + int(b == 2))

    def wait_partner_first(self):
        low = PARTS[0][1]
        assert 28 * low == 4 * (TILES - low)
        self.wait(self.qbuf.at[:, 0, 0, 1, slice(low, TILES)], self.cross_sem.at[0])

    def wait_partner(self, wave):
        ys, zs = (slice(0, 3), slice(0, 3), slice(0, 1))[wave], (slice(0, 3), slice(0, 2), slice(0, 1))[wave]
        ref = self.qbuf.at[:, ys, zs, 1, slice(PARTS[0][1] if wave else 0, TILES)]
        self.wait(ref, self.cross_sem.at[wave + 1])

    def drain(self):
        rest = slice(1, SIDE)
        for ref in (
            self.qbuf.at[rest], self.qbuf.at[0, rest], self.qbuf.at[0, 0, rest], self.qbuf.at[0, 0, 0, 1]
        ):
            pltpu.make_async_copy(ref, ref, self.send_sem).wait()


def kernel(
    q_hbm, docs_hbm, lengths_hbm, sdev_hbm, slist_hbm, srow_hbm, pdev_hbm, plist_hbm,
    out_ref,
    lengths, sdev_ref, slist_ref, srow_ref, pdev_ref, plist_ref,
    qbuf, docs, dpre, gath, oh, sel, slot_ref, psel, ask, asked, psend, precv, rsend, rrecv,
    known, small_sem, load_sem, gsend, grecv, gcross, xsend, xrecv,
):
    me = coords()
    own_number = (me[0] * SIDE + me[1]) * 8 + me[2] * 2 + me[3]
    peers = Peers(me)
    barrier = pltpu.get_barrier_semaphore()
    small = [
        pltpu.make_async_copy(src, dst, small_sem.at[n])
        for n, (src, dst) in enumerate((
            (sdev_hbm, sdev_ref), (slist_hbm, slist_ref), (srow_hbm, srow_ref),
            (pdev_hbm, pdev_ref), (plist_hbm, plist_ref), (lengths_hbm, lengths),
        ))
    ]
    for copy in small:
        copy.start()

    gather = Gather(qbuf, gsend, grecv, gcross, me)
    lines = [[gather.peers[axis, step] for step in (2, 1, 3)] for axis in range(3)]

    def tell(sem, them):
        for peer in them:
            pl.semaphore_signal(sem, inc=1, device_id=peer, device_id_type=MESH)

    others = [(gx, gather.partner[1]) for gx, _ in lines[0]] + [gather.partner]
    tell(barrier, lines[0] + others + lines[1] + lines[2])

    for t in range(TILES):
        pltpu.make_async_copy(
            q_hbm.at[:, pl.ds(t * 128, 128)], qbuf.at[0, 0, 0, 0, t], load_sem.at[0]
        ).start()

    docs_copy = pltpu.make_async_copy(docs_hbm.at[:, pl.ds(0, ELIG), :], docs, load_sem.at[1])
    docs_copy.start()
    dpre_copy = pltpu.make_async_copy(docs_hbm.at[:, :, pl.ds(0, PREFIX)], dpre, load_sem.at[2])
    dpre_copy.start()
    for copy in small:
        copy.wait()

    dev = iota((QROWS, DEVS), 1)
    sdev = sdev_ref[...]
    scode = (slist_ref[...] * ELIG + srow_ref[...] + 1).astype(F32)
    pdev = pdev_ref[...]
    pcode = (plist_ref[...] + 1).astype(F32)
    lower = (iota((QROWS, QROWS), 1) < iota((QROWS, QROWS), 0)).astype(F32).astype(BF16)
    qnum = iota((QROWS, DEVS), 0).astype(F32) + 1.0

    def table(devs, codes, width):
        got = jnp.zeros((QROWS, DEVS), F32)
        for s in range(width):
            got = got + jnp.where(devs[:, s : s + 1] == dev, codes[:, s : s + 1], 0.0)
        used = jnp.where(got > 0.0, 1.0, 0.0)
        rank = jnp.dot(lower, used.astype(BF16), preferred_element_type=F32)
        return got, jnp.where(used > 0.0, rank, -1.0)

    stab, srank = table(sdev, scode, SHORT)
    ptab, prank = table(pdev, pcode, PROBES)
    krow = iota((16, DEVS), 0)
    slots = jnp.zeros((16, DEVS), F32)
    for base, row_base, tab, rank, cap in (
        (LANE_CODE, LANE_ROW, stab, srank, CAP),
        (LANE_LIST, LANE_PROW, ptab, prank, PCAP),
    ):
        for j in range(cap):
            hit = rank == float(j)
            code = jnp.sum(jnp.where(hit, tab, 0.0), axis=0, keepdims=True) - 1.0
            row = jnp.sum(jnp.where(hit, qnum, 0.0), axis=0, keepdims=True) - 1.0
            slots = jnp.where(krow == base + j, code, slots)
            slots = jnp.where(krow == row_base + j, row, slots)
    slots = jnp.concatenate([slots, jnp.zeros((112, DEVS), F32)], axis=0).T
    ask[...] = slots.astype(I32).reshape(DEVS, 1, DEVS)

    pltpu.make_async_copy(qbuf.at[0, 0, 0, 1], qbuf.at[0, 0, 0, 0], load_sem.at[0]).wait()
    pl.semaphore_wait(barrier, 13)
    tell(known.at[0], lines[1])
    gather.begin()
    def exchange_rows(src, dst, peer, number):
        pltpu.make_async_remote_copy(
            src_ref=src, dst_ref=dst, send_sem=xsend.at[number], recv_sem=xrecv.at[number],
            device_id=peer, device_id_type=MESH,
        ).start()

    def exchanged(send, recv, number, rows):
        some = pl.ds(0, rows)
        pltpu.make_async_copy(recv.at[some], recv.at[some], xrecv.at[number]).wait()
        pltpu.make_async_copy(send.at[some], send.at[some], xsend.at[number]).wait()

    def ask_peer(peer, flat, off, back):
        exchange_rows(ask.at[flat], asked.at[back], peer, back % CHIPS // HALF)


    lane = iota((16, DEVS), 1)

    def read_slots(half):
        exchanged(ask, asked, half, DEVS // 2 - (half == 0))
        if half == 0:
            asked[0] = ask[own_number]
        for core in range(2):
            here = pl.ds(core * CHIPS + half * HALF, HALF)
            slot_ref[here] = asked[here].reshape(HALF, DEVS)
        doc_number = iota((HALF, LISTS * ELIG), 1)
        for j in range(CAP):
            for core in range(2):
                here = pl.ds(core * CHIPS + half * HALF, HALF)
                hit = slot_ref[here, LANE_CODE + j : LANE_CODE + j + 1] == doc_number
                oh[half, pl.ds((j * 2 + core) * HALF, HALF), :] = jnp.where(hit, 1.0, 0.0).astype(BF16)

    def pick(half, low, high):
        def body(n, carry):
            cols = pl.ds(pl.multiple_of(n * 256, 256), 256)
            block = docs[:, :, cols].reshape(LISTS * ELIG, 256)
            got = jnp.dot(oh[half], block, preferred_element_type=F32)
            gath[:, :, pl.ds(half * HALF, HALF), cols] = got.astype(BF16).reshape(CAP, 2, HALF, 256)
            return carry

        lax.fori_loop(low, high, body, 0, unroll=2)

    group_row = iota((16, 1), 0)
    group_col = iota((16, 256), 1)

    def blocks(start, stop, low, high):
        places = [(*BLOCKS[off % CHIPS], off // CHIPS) for off in range(start, stop)]
        tiles = [
            jnp.concatenate([qbuf[y, x, z, c, t] for y, x, z, c in places], axis=0)
            for t in range(low, high)
        ]
        return jnp.concatenate(tiles, axis=1)

    def queries(g, low, high):
        return blocks(g * 16, g * 16 + 16, low, high)

    def column(g, at):
        number = slot_ref[pl.ds(g * 16, 16), at : at + 1]
        return jnp.where(number < 0, -1, group_row * QROWS + number)

    def prefix_scores():
        for g in range(2 * SIDE):
            hits = [jnp.where(column(g, LANE_PROW + p) == group_col, 1.0, 0.0) for p in range(PCAP)]
            hit = jnp.concatenate(hits, axis=0).astype(BF16)
            rows = jnp.dot(hit, queries(g, 0, PREFIX // 128), preferred_element_type=F32)
            norm = jnp.sqrt(1.0 + jnp.sum(rows * rows, axis=1, keepdims=True))
            rows = rows / norm
            for p in range(PCAP):
                psel[pl.ds(p * DEVS + g * 16, 16), :] = rows[p * 16 : (p + 1) * 16, :]
        slot_t = slot_ref[...].astype(F32).T
        lists = jnp.concatenate(
            [slot_t[LANE_LIST + p : LANE_LIST + p + 1, :] for p in range(PCAP)], axis=1
        )
        wanted = psel[...].T.astype(BF16)
        sel[...] = jnp.zeros_like(sel)
        for n in range(LISTS):
            got = jnp.dot(dpre[n], wanted, preferred_element_type=F32)
            sel[...] = jnp.where(lists == float(n), got, sel[...])
        rows_valid = jnp.zeros((1, PCAP * DEVS), I32)
        for n in range(LISTS):
            rows_valid = jnp.where(lists == float(n), lengths[n], rows_valid)
        sub = iota((8, DEVS), 0)
        tops = []
        for p in range(PCAP):
            lanes = pl.ds(p * DEVS, DEVS)
            bound = rows_valid[:, p * DEVS : (p + 1) * DEVS]
            seq = [
                jnp.where(sub + v * 8 < bound, sel[pl.ds(v * 8, 8), lanes], LOW) for v in range(32)
            ]
            seq = sort_down(seq)
            for shift in (4, 2, 1):
                seq = join_rolled(seq, shift, 0)
            for m in range(TOPK // 8):
                block = seq[m * 8]
                for s in range(1, 8):
                    block = jnp.where(sub == s, seq[m * 8 + s], block)
                tops.append(block)
        tops.append(jnp.zeros((DEVS - PCAP * TOPK, DEVS), F32))
        psend[...] = jnp.concatenate(tops, axis=0).T.reshape(DEVS, 1, DEVS)

    def return_prefix():
        peers.each(lambda peer, flat, off, back: exchange_rows(psend.at[off], precv.at[own_number], peer, 2))

    def merge_prefix():
        exchanged(psend, precv, 2, DEVS - 1)
        precv[own_number] = psend[0]
        back = precv[...].reshape(DEVS, DEVS).T
        first, second = prank == 0.0, prank == 1.0
        seq = [
            jnp.where(
                first, back[k : k + 1, :], jnp.where(second, back[TOPK + k : TOPK + k + 1, :], LOW)
            )
            for k in range(TOPK)
        ]
        for shift in (64, 32, 16, 8, 4, 2, 1):
            seq = join_rolled(seq, shift, 1)
        best = seq[0]
        for k in range(1, TOPK):
            best = jnp.where(lane == k, seq[k], best)
        out_ref[...] = best

    def rescore(wave, core):
        start, stop = WAVES[wave]
        low, high = start // 16 * 16, -(-stop // 16) * 16
        rows, cols = high - low, (stop - start) * QROWS
        left = gath[:, core, pl.ds(low, rows), :].reshape(CAP * rows, FULL)
        start, stop, low = start + core * CHIPS, stop + core * CHIPS, low + core * CHIPS
        got = lax.dot_general(
            left, blocks(start, stop, 0, TILES), (((1,), (1,)), ((), ())), preferred_element_type=F32
        )
        base = (iota((rows, 1), 0) + (low - start)) * QROWS
        col = iota((rows, cols), 1)
        total = jnp.zeros((rows, cols), F32)
        for j in range(CAP):
            number = slot_ref[pl.ds(low, rows), LANE_ROW + j : LANE_ROW + j + 1]
            hit = jnp.where(number < 0, -1, base + number) == col
            total = total + jnp.where(hit, got[j * rows : (j + 1) * rows, :], 0.0)
        value = jnp.sum(total, axis=0, keepdims=True)
        rest = WAVE_ROWS[wave] * 128 - cols
        value = jnp.concatenate([value, jnp.zeros((1, rest), F32)], axis=1)
        to = core * sum(WAVE_ROWS) + sum(WAVE_ROWS[:wave])
        for n in range(WAVE_ROWS[wave]):
            rsend[to + n] = value[:, n * 128 : (n + 1) * 128]
        for off in range(start, stop):
            if off:
                exchange_rows(rsend.at[to + (off - start) // 8], rrecv.at[own_number], peers.at(off), 3)

    first, others = gather.parts[:1], gather.parts[1:]
    pl.semaphore_wait(known.at[0], 3)
    tell(known.at[1], lines[2])
    gather.first_axis(first)
    gather.first_axis(others)
    pl.semaphore_wait(known.at[1], 3)
    peers.each(ask_peer, near_half_first=True)
    gather.home_blocks(first)
    gather.home_blocks(others)
    docs_copy.wait()
    dpre_copy.wait()
    gather.second_axis(first)
    gather.second_axis(others)
    gather.third_axis_line(first)
    gather.second_axis_end(first)
    gather.third_axis_line(others)
    read_slots(0)
    pick(0, 0, 2)
    gather.second_axis_end(others)
    gather.third_axis(first, NEAR)
    read_slots(1)
    pick(0, 2, 8)
    gather.third_axis(others, NEAR)
    pick(1, 0, 4)
    gather.third_axis(first, FAR)
    gather.third_axis_line_end(first)
    pick(1, 4, 8)
    gather.third_axis(others, FAR)
    gather.third_axis_end(first, NEAR)
    gather.third_axis_end(first, FAR)
    rescore(0, 0)
    gather.wait_partner(0)
    rescore(0, 1)
    gather.third_axis_line_end(others)
    gather.third_axis_end(others, NEAR)
    gather.wait_partner_first()
    prefix_scores()
    return_prefix()
    gather.third_axis_end(others, FAR)
    rescore(1, 0)
    rescore(2, 0)
    gather.wait_partner(1)
    rescore(1, 1)
    gather.wait_partner(2)
    rescore(2, 1)
    gather.drain()
    merge_prefix()
    exchanged(rrecv, rrecv, 3, DEVS - 1)
    squares = jnp.zeros((QROWS, 128), F32)
    for t in range(TILES):
        value = qbuf[0, 0, 0, 0, t].astype(F32)
        squares = squares + value * value
    full_norm = jnp.sqrt(1.0 + jnp.sum(squares, axis=1, keepdims=True))
    rrecv[own_number] = rsend[0]
    back = rrecv[...].reshape(DEVS, DEVS).T
    other = iota((16, DEVS), 1)
    seen = (me[0] + SIDE - other // 32) % SIDE * 16 + (me[1] + SIDE - other // 8 % SIDE) % SIDE * 4
    seen = seen + (me[2] + SIDE - other // 2 % SIDE) % SIDE
    place = jnp.zeros((QROWS, DEVS), I32)
    for low, high in WAVES:
        for n in range(low, high):
            y, x, z = BLOCKS[n]
            place = jnp.where(seen == y * 16 + x * 4 + z, (n - low) % 8, place)
    value = jnp.zeros((QROWS, DEVS), F32)
    for n in range(8):
        value = jnp.where(place == n, back[n * 16 : (n + 1) * 16, :], value)
    out = jnp.zeros((QROWS, DEVS), F32)
    for s in range(SHORT):
        one = jnp.sum(jnp.where(sdev[:, s : s + 1] == dev, value, 0.0), axis=1, keepdims=True)
        out = jnp.where(lane == s, one, out)
    out_ref[:, pl.ds(TOPK, SHORT)] = (out / full_norm)[:, :SHORT]


def shards(queries, probe_dev, probe_list, documents, lengths, short_dev, short_list, short_row):
    vmem = pl.BlockSpec(memory_space=pltpu.VMEM)
    anywhere = pl.BlockSpec(memory_space=pl.ANY)
    out = pl.pallas_call(
        kernel,
        name="search",
        out_shape=pltpu.VMEM((QROWS, DEVS), F32),
        in_specs=[anywhere] * 8,
        out_specs=vmem,
        scratch_shapes=[
            pltpu.SMEM((LISTS,), I32),
            pltpu.VMEM((QROWS, SHORT), I32),
            pltpu.VMEM((QROWS, SHORT), I32),
            pltpu.VMEM((QROWS, SHORT), I32),
            pltpu.VMEM((QROWS, PROBES), I32),
            pltpu.VMEM((QROWS, PROBES), I32),
            pltpu.VMEM((SIDE, SIDE, SIDE, 2, TILES, QROWS, 128), BF16),
            pltpu.VMEM((LISTS, ELIG, FULL), BF16),
            pltpu.VMEM((LISTS, ROWS, PREFIX), BF16),
            pltpu.VMEM((CAP, 2, CHIPS, FULL), BF16),
            pltpu.VMEM((2, CAP * CHIPS, LISTS * ELIG), BF16),
            pltpu.VMEM((ROWS, PCAP * DEVS), F32),
            pltpu.VMEM((DEVS, DEVS), I32),
            pltpu.VMEM((PCAP * DEVS, PREFIX), F32),
            pltpu.VMEM((DEVS, 1, DEVS), I32),
            pltpu.VMEM((DEVS, 1, DEVS), I32),
            pltpu.VMEM((DEVS, 1, DEVS), F32),
            pltpu.VMEM((DEVS, 1, DEVS), F32),
            pltpu.VMEM((2 * sum(WAVE_ROWS), 1, DEVS), F32),
            pltpu.VMEM((DEVS, 1, DEVS), F32),
            pltpu.SemaphoreType.REGULAR((2,)),
            pltpu.SemaphoreType.DMA((6,)),
            pltpu.SemaphoreType.DMA((3,)),
            pltpu.SemaphoreType.DMA,
            pltpu.SemaphoreType.DMA((11 * len(PARTS),)),
            pltpu.SemaphoreType.DMA((4,)),
            pltpu.SemaphoreType.DMA((4,)),
            pltpu.SemaphoreType.DMA((4,)),
        ],
        compiler_params=pltpu.CompilerParams(
            collective_id=0, has_side_effects=True, vmem_limit_bytes=60 * 1024 * 1024
        ),
    )(queries, documents, lengths, short_dev, short_list, short_row, probe_dev, probe_list)
    return out[:, :TOPK], out[:, TOPK : TOPK + SHORT]


def solution(mesh):
    spread = P(("gx", "gy"), None)
    in_specs = (spread, spread, spread, P(("gx", "gy"), None, None), P(("gx", "gy")), spread, spread, spread)
    return jax.shard_map(shards, mesh=mesh, in_specs=in_specs, out_specs=(spread, spread), check_vma=False)
```

time: 46.6 us -> 42.9 us (0.921)
  Pallas kernels: 45.1 us -> 41.4 us
    pallas_call x1, Pallas kernels: 45.1 us -> 41.4 us  [shards(): pl.pallas_call(kernel, name='search', out_shape=pltpu.VMEM((QROWS, DEVS),...]
where the time goes in v4:
time: 42.9 us; the launch traced here: 42.7 us
  Pallas kernels  41.4 us (97%)
  local copies, waits for them, and re-layouts  0.67 us (2%)
  between operations  0.64 us (1%)
    pallas_call x1, Pallas kernels, shards(): pl.pallas_call(kernel, name='search', out_shape=pltpu.VMEM((QROWS, DEVS),...  41.4 us

profile of v4, /device:TPU:1, one launch (start us, length us, event | category | flops | bytes accessed | tf_op | source)
XLA Modules:
  0.0 42.7 jit_solution(18102365673514710694)
XLA Ops:
  0.6 41.4 %search.1 = f32[16,128]{1,0:T(8,128)S(1)} custom-call(bf16[16,2048]{1,0:T(8,128)(2,1)} %q_hbm.1, bf16[16,256,2048]{2,1,0:T(8,128)(2,1)} %docs_hbm.1, s32[16]{0:T(128)} %lengths_hbm.1, s32[16,32]{1,0:T(8,128)} %sdev_hbm.1, s32[16,32]{1,0:T(8,128)} %slist_hbm.1, s32[16,32]{1,0:T(8,128)} %srow_hbm.1, s32[16,16]{1,0:T(8,128)} %pdev_hbm.1, s32[16,16]{1,0:T(8,128)} %plist_hbm.1), custom_call_target="tpu_custom_call" | custom-call | tf_op jit(solution)/shard_map/search/pallas_call | solution.py:579
  42.1 0.7 %fusion = (f32[16,32]{1,0:T(8,128)}, f32[16,32]{1,0:T(8,128)}) fusion(f32[16,128]{1,0:T(8,128)S(1)} %search.1), kind=kLoop, calls=%fused_computation | loop fusion | bytes 8192 | tf_op jit(solution)/shard_map/slice | solution.py:619

commit v5 on v4

--- a/solution.py
+++ b/solution.py
@@ -285,6 +285,20 @@
     own_number = (me[0] * SIDE + me[1]) * 8 + me[2] * 2 + me[3]
     peers = Peers(me)
     barrier = pltpu.get_barrier_semaphore()
+    gather = Gather(qbuf, gsend, grecv, gcross, me)
+    lines = [[gather.peers[axis, step] for step in (2, 1, 3)] for axis in range(3)]
+
+    def tell(sem, them):
+        for peer in them:
+            pl.semaphore_signal(sem, inc=1, device_id=peer, device_id_type=MESH)
+
+    others = [(gx, gather.partner[1]) for gx, _ in lines[0]] + [gather.partner]
+    tell(barrier, lines[0] + others + lines[1] + lines[2])
+
+    for t in range(TILES):
+        pltpu.make_async_copy(
+            q_hbm.at[:, pl.ds(t * 128, 128)], qbuf.at[0, 0, 0, 0, t], load_sem.at[0]
+        ).start()
     small = [
         pltpu.make_async_copy(src, dst, small_sem.at[n])
         for n, (src, dst) in enumerate((
@@ -294,26 +308,15 @@
     ]
     for copy in small:
         copy.start()
-
-    gather = Gather(qbuf, gsend, grecv, gcross, me)
-    lines = [[gather.peers[axis, step] for step in (2, 1, 3)] for axis in range(3)]
-
-    def tell(sem, them):
-        for peer in them:
-            pl.semaphore_signal(sem, inc=1, device_id=peer, device_id_type=MESH)
-
-    others = [(gx, gather.partner[1]) for gx, _ in lines[0]] + [gather.partner]
-    tell(barrier, lines[0] + others + lines[1] + lines[2])
-
-    for t in range(TILES):
-        pltpu.make_async_copy(
-            q_hbm.at[:, pl.ds(t * 128, 128)], qbuf.at[0, 0, 0, 0, t], load_sem.at[0]
-        ).start()
-
     docs_copy = pltpu.make_async_copy(docs_hbm.at[:, pl.ds(0, ELIG), :], docs, load_sem.at[1])
     docs_copy.start()
     dpre_copy = pltpu.make_async_copy(docs_hbm.at[:, :, pl.ds(0, PREFIX)], dpre, load_sem.at[2])
     dpre_copy.start()
+
+    pltpu.make_async_copy(qbuf.at[0, 0, 0, 1], qbuf.at[0, 0, 0, 0], load_sem.at[0]).wait()
+    pl.semaphore_wait(barrier, 13)
+    tell(known.at[0], lines[1])
+    gather.begin()
     for copy in small:
         copy.wait()
 
@@ -350,10 +353,6 @@
     slots = jnp.concatenate([slots, jnp.zeros((112, DEVS), F32)], axis=0).T
     ask[...] = slots.astype(I32).reshape(DEVS, 1, DEVS)
 
-    pltpu.make_async_copy(qbuf.at[0, 0, 0, 1], qbuf.at[0, 0, 0, 0], load_sem.at[0]).wait()
-    pl.semaphore_wait(barrier, 13)
-    tell(known.at[0], lines[1])
-    gather.begin()
     def exchange_rows(src, dst, peer, number):
         pltpu.make_async_remote_copy(
             src_ref=src, dst_ref=dst, send_sem=xsend.at[number], recv_sem=xrecv.at[number],
@@ -387,13 +386,13 @@
 
     def pick(half, low, high):
         def body(n, carry):
-            cols = pl.ds(pl.multiple_of(n * 256, 256), 256)
-            block = docs[:, :, cols].reshape(LISTS * ELIG, 256)
+            cols = pl.ds(pl.multiple_of(n * 512, 512), 512)
+            block = docs[:, :, cols].reshape(LISTS * ELIG, 512)
             got = jnp.dot(oh[half], block, preferred_element_type=F32)
-            gath[:, :, pl.ds(half * HALF, HALF), cols] = got.astype(BF16).reshape(CAP, 2, HALF, 256)
+            gath[:, :, pl.ds(half * HALF, HALF), cols] = got.astype(BF16).reshape(CAP, 2, HALF, 512)
             return carry
 
-        lax.fori_loop(low, high, body, 0, unroll=2)
+        lax.fori_loop(low, high, body, 0)
 
     group_row = iota((16, 1), 0)
     group_col = iota((16, 256), 1)
@@ -520,17 +519,17 @@
     pick(0, 0, 2)
     gather.second_axis_end(others)
     gather.third_axis(first, NEAR)
+    pick(0, 2, 4)
     read_slots(1)
-    pick(0, 2, 8)
+    pick(1, 0, 2)
     gather.third_axis(others, NEAR)
-    pick(1, 0, 4)
     gather.third_axis(first, FAR)
     gather.third_axis_line_end(first)
-    pick(1, 4, 8)
-    gather.third_axis(others, FAR)
+    pick(1, 2, 4)
+    rescore(0, 0)
     gather.third_axis_end(first, NEAR)
     gather.third_axis_end(first, FAR)
-    rescore(0, 0)
+    gather.third_axis(others, FAR)
     gather.wait_partner(0)
     rescore(0, 1)
     gather.third_axis_line_end(others)
@@ -539,22 +538,19 @@
     prefix_scores()
     return_prefix()
     gather.third_axis_end(others, FAR)
+    rescore(2, 0)
     rescore(1, 0)
-    rescore(2, 0)
     gather.wait_partner(1)
-    rescore(1, 1)
     gather.wait_partner(2)
     rescore(2, 1)
+    rescore(1, 1)
     gather.drain()
     merge_prefix()
-    exchanged(rrecv, rrecv, 3, DEVS - 1)
     squares = jnp.zeros((QROWS, 128), F32)
     for t in range(TILES):
         value = qbuf[0, 0, 0, 0, t].astype(F32)
         squares = squares + value * value
     full_norm = jnp.sqrt(1.0 + jnp.sum(squares, axis=1, keepdims=True))
-    rrecv[own_number] = rsend[0]
-    back = rrecv[...].reshape(DEVS, DEVS).T
     other = iota((16, DEVS), 1)
     seen = (me[0] + SIDE - other // 32) % SIDE * 16 + (me[1] + SIDE - other // 8 % SIDE) % SIDE * 4
     seen = seen + (me[2] + SIDE - other // 2 % SIDE) % SIDE
@@ -563,6 +559,9 @@
         for n in range(low, high):
             y, x, z = BLOCKS[n]
             place = jnp.where(seen == y * 16 + x * 4 + z, (n - low) % 8, place)
+    exchanged(rrecv, rrecv, 3, DEVS - 1)
+    rrecv[own_number] = rsend[0]
+    back = rrecv[...].reshape(DEVS, DEVS).T
     value = jnp.zeros((QROWS, DEVS), F32)
     for n in range(8):
         value = jnp.where(place == n, back[n * 16 : (n + 1) * 16, :], value)

time: 42.9 us -> 41.6 us (0.970)
  Pallas kernels: 41.4 us -> 40.2 us
    pallas_call x1, Pallas kernels: 41.4 us -> 40.2 us  [shards(): pl.pallas_call(kernel, name='search', out_shape=pltpu.VMEM((QROWS, DEVS),...]
where the time goes in v5:
time: 41.6 us; the launch traced here: 41.5 us
  Pallas kernels  40.2 us (97%)
  local copies, waits for them, and re-layouts  0.67 us (2%)
  between operations  0.64 us (2%)
    pallas_call x1, Pallas kernels, shards(): pl.pallas_call(kernel, name='search', out_shape=pltpu.VMEM((QROWS, DEVS),...  40.2 us

profile of v5, /device:TPU:1, one launch (start us, length us, event | category | flops | bytes accessed | tf_op | source)
XLA Modules:
  0.0 41.5 jit_solution(14951806634374064156)
XLA Ops:
  0.6 40.2 %search.1 = f32[16,128]{1,0:T(8,128)S(1)} custom-call(bf16[16,2048]{1,0:T(8,128)(2,1)} %q_hbm.1, bf16[16,256,2048]{2,1,0:T(8,128)(2,1)} %docs_hbm.1, s32[16]{0:T(128)} %lengths_hbm.1, s32[16,32]{1,0:T(8,128)} %sdev_hbm.1, s32[16,32]{1,0:T(8,128)} %slist_hbm.1, s32[16,32]{1,0:T(8,128)} %srow_hbm.1, s32[16,16]{1,0:T(8,128)} %pdev_hbm.1, s32[16,16]{1,0:T(8,128)} %plist_hbm.1), custom_call_target="tpu_custom_call" | custom-call | tf_op jit(solution)/shard_map/search/pallas_call | solution.py:578
  40.8 0.7 %fusion = (f32[16,32]{1,0:T(8,128)}, f32[16,32]{1,0:T(8,128)}) fusion(f32[16,128]{1,0:T(8,128)S(1)} %search.1), kind=kLoop, calls=%fused_computation | loop fusion | bytes 8192 | tf_op jit(solution)/shard_map/slice | solution.py:618

commit v6 on v5

--- a/solution.py
+++ b/solution.py
@@ -386,10 +386,10 @@
 
     def pick(half, low, high):
         def body(n, carry):
-            cols = pl.ds(pl.multiple_of(n * 512, 512), 512)
-            block = docs[:, :, cols].reshape(LISTS * ELIG, 512)
+            cols = pl.ds(pl.multiple_of(n * 1024, 1024), 1024)
+            block = docs[:, :, cols].reshape(LISTS * ELIG, 1024)
             got = jnp.dot(oh[half], block, preferred_element_type=F32)
-            gath[:, :, pl.ds(half * HALF, HALF), cols] = got.astype(BF16).reshape(CAP, 2, HALF, 512)
+            gath[:, :, pl.ds(half * HALF, HALF), cols] = got.astype(BF16).reshape(CAP, 2, HALF, 1024)
             return carry
 
         lax.fori_loop(low, high, body, 0)
@@ -516,16 +516,16 @@
     gather.second_axis_end(first)
     gather.third_axis_line(others)
     read_slots(0)
-    pick(0, 0, 2)
+    pick(0, 0, 1)
     gather.second_axis_end(others)
     gather.third_axis(first, NEAR)
-    pick(0, 2, 4)
+    pick(0, 1, 2)
     read_slots(1)
-    pick(1, 0, 2)
+    pick(1, 0, 1)
     gather.third_axis(others, NEAR)
     gather.third_axis(first, FAR)
     gather.third_axis_line_end(first)
-    pick(1, 2, 4)
+    pick(1, 1, 2)
     rescore(0, 0)
     gather.third_axis_end(first, NEAR)
     gather.third_axis_end(first, FAR)
@@ -534,12 +534,12 @@
     rescore(0, 1)
     gather.third_axis_line_end(others)
     gather.third_axis_end(others, NEAR)
+    rescore(1, 0)
     gather.wait_partner_first()
     prefix_scores()
+    gather.third_axis_end(others, FAR)
     return_prefix()
-    gather.third_axis_end(others, FAR)
     rescore(2, 0)
-    rescore(1, 0)
     gather.wait_partner(1)
     gather.wait_partner(2)
     rescore(2, 1)

time: 41.6 us -> 41.5 us (level)
  no operation moved by 1% of the time
where the time goes in v6:
time: 41.5 us; the launch traced here: 41.4 us
  Pallas kernels  40.1 us (97%)
  local copies, waits for them, and re-layouts  0.67 us (2%)
  between operations  0.64 us (2%)
    pallas_call x1, Pallas kernels, shards(): pl.pallas_call(kernel, name='search', out_shape=pltpu.VMEM((QROWS, DEVS),...  40.1 us

profile of v6, /device:TPU:1, one launch (start us, length us, event | category | flops | bytes accessed | tf_op | source)
XLA Modules:
  0.0 41.4 jit_solution(4559593010496691166)
XLA Ops:
  0.6 40.1 %search.1 = f32[16,128]{1,0:T(8,128)S(1)} custom-call(bf16[16,2048]{1,0:T(8,128)(2,1)} %q_hbm.1, bf16[16,256,2048]{2,1,0:T(8,128)(2,1)} %docs_hbm.1, s32[16]{0:T(128)} %lengths_hbm.1, s32[16,32]{1,0:T(8,128)} %sdev_hbm.1, s32[16,32]{1,0:T(8,128)} %slist_hbm.1, s32[16,32]{1,0:T(8,128)} %srow_hbm.1, s32[16,16]{1,0:T(8,128)} %pdev_hbm.1, s32[16,16]{1,0:T(8,128)} %plist_hbm.1), custom_call_target="tpu_custom_call" | custom-call | tf_op jit(solution)/shard_map/search/pallas_call | solution.py:578
  40.8 0.7 %fusion = (f32[16,32]{1,0:T(8,128)}, f32[16,32]{1,0:T(8,128)}) fusion(f32[16,128]{1,0:T(8,128)S(1)} %search.1), kind=kLoop, calls=%fused_computation | loop fusion | bytes 8192 | tf_op jit(solution)/shard_map/slice | solution.py:618
